TPU v7x, 256 devices: a whole 4x4x8 slice. The times are simulated.
256 devices in a mesh: dp: 8 (over y, x_lo), tensor: 16 (over z, core), fisher: 2 (over x_hi).
Axes of the slice: x: 4 (x_hi: 2, x_lo: 2; x = x_hi * 2 + x_lo), y: 4, z: 8, core: 2. Of those that a mesh axis runs over, the one named last changes fastest.
Arguments:
- train_inputs: bfloat16 [176, 257, 1280], P('dp', None, 'fisher'), may hold values from -6 to 6
- train_cotangents: bfloat16 [176, 257, 3840], P('dp', None, 'tensor'), may hold values from -6 to 6
- train_ids: int32 [176], P('dp'), may hold values from 0 to 63
- query_projection_inputs: bfloat16 [16, 257, 1280], P('tensor', None, 'fisher'), may hold values from -6 to 6
- query_output_cotangents: bfloat16 [16, 257, 3840], P('tensor'), may hold values from -6 to 6
- query_ids: int32 [16], replicated, may hold values from 0 to 15
- fisher_diagonal_weight: bfloat16 [2, 3840, 1280], P(None, 'tensor', 'fisher'), may hold values from 0.049804688 to 2
- layer_index: int32 [16], replicated, may hold values from 0 to 1
Outputs:
- influence: float32 [64, 16, 16], P(('dp', 'fisher'), None, 'tensor')
All inputs are finite; a program needn't handle non-finite values.
Results may differ from a plain program's by a relative error of at most 0.004.
Values may be sent and summed in bfloat16 or wider, within the bound.
No kernel may reach another device: no remote copies, remote signals or barrier semaphores. Data moves between devices by JAX's collectives and lax.ppermute only.
A program may use at most 128 MiB of HBM per device.

v0:
```python
import functools
import math

import jax
import jax.numpy as jnp
from jax import lax
from jax.experimental import pallas as pl
from jax.experimental.pallas import tpu as pltpu
from jax.sharding import Mesh, PartitionSpec as P

D = 1280
HEAD_DIM = 80
SEQ = 257
BODY = 256
TIDS = 64
QIDS = 16
HW = 3 * HEAD_DIM
HALF = D // 2
ROWS = 16
NY, NXL, NZ, NC, NXH = 4, 2, 8, 2, 2
AXES = ("y", "xlo", "z", "core", "xhi")
CUTS = (11, 11)
SCALE = 1.0 / (SEQ * math.sqrt(HW * D))
ANY = pl.BlockSpec(memory_space=pl.ANY)
VMEM = pl.BlockSpec(memory_space=pltpu.VMEM)
SMEM = pl.BlockSpec(memory_space=pltpu.SMEM)


def flat(y, x, z, c):
    return (((y % 4) * NXL + (x % 4) % 2) * NZ + z % NZ) * NC * NXH + (c % 2) * NXH + (x % 4) // 2


def send(value, to):
    places = [(y, x, z, c) for y in range(4) for x in range(4) for z in range(NZ) for c in range(2)]
    return lax.ppermute(value, AXES, [(flat(*p), flat(*to(*p))) for p in places])


def outer_sum(cot, act):
    body = lax.dot_general(
        cot[:BODY], act[:BODY], (((0,), (0,)), ((), ())), preferred_element_type=jnp.float32
    )
    column = jnp.transpose(cot[BODY:SEQ].astype(jnp.float32))
    return body + column * act[BODY:SEQ].astype(jnp.float32)


def train_kernel(first, group, cot_hbm, act_hbm, out_ref, cot, act, sems):
    count = out_ref.shape[0]
    copies = []
    for i in range(0, count, group):
        size = min(group, count - i)
        src, dst = pl.ds(first + i, size), pl.ds(i, size)
        pair = (
            pltpu.make_async_copy(cot_hbm.at[src], cot.at[dst], sems.at[0, i // group]),
            pltpu.make_async_copy(act_hbm.at[src], act.at[dst], sems.at[1, i // group]),
        )
        copies.append((i, size, pair))
        for c in pair:
            c.start()
    for i, size, pair in copies:
        for c in pair:
            c.wait()
        for j in range(i, i + size):
            out_ref[j] = outer_sum(cot[j], act[j]).astype(jnp.bfloat16)


def train_grad(cot, act, first, count):
    group = 2
    return pl.pallas_call(
        functools.partial(train_kernel, first, group),
        in_specs=[ANY, ANY],
        out_specs=VMEM,
        out_shape=jax.ShapeDtypeStruct((count, HW, HALF), jnp.bfloat16),
        scratch_shapes=[
            pltpu.VMEM((count, SEQ, HW), jnp.bfloat16),
            pltpu.VMEM((count, SEQ, HALF), jnp.bfloat16),
            pltpu.SemaphoreType.DMA((2, -(-count // group))),
        ],
        name="train_grad",
        compiler_params=pltpu.CompilerParams(vmem_limit_bytes=58 * 2**20),
        cost_estimate=pl.CostEstimate(
            flops=2 * count * HW * HALF * SEQ * 4,
            bytes_accessed=2 * count * (SEQ * (HW + HALF) + HW * HALF),
            transcendentals=0,
        ),
    )(cot, act)


def stack_kernel(*refs):
    *sources, out = refs
    for i, ref in enumerate(sources):
        out[i] = ref[...]


def stack(*parts):
    return pl.pallas_call(
        stack_kernel,
        in_specs=[VMEM] * len(parts),
        out_specs=VMEM,
        out_shape=jax.ShapeDtypeStruct((len(parts),) + parts[0].shape, parts[0].dtype),
        name="stack",
        compiler_params=pltpu.CompilerParams(vmem_limit_bytes=4 * 2**20),
    )(*parts)


def pair_kernel(count_train, *refs):
    acts, refs = refs[:8], refs[8:]
    cots, refs = refs[:8], refs[8:]
    grads, refs = refs[:4], refs[4:]
    own_fisher, other_fisher, ids_ref, query_ids, layer_index, out_ref = refs[:6]
    cot, grad, weighted, act, sems = refs[6:]
    core, z, y = lax.axis_index("core"), lax.axis_index("z"), lax.axis_index("y")
    x = lax.axis_index("xhi") * 2 + lax.axis_index("xlo")
    first, later = [], []
    for k, ref in enumerate(acts):
        first.append(pltpu.make_async_copy(ref, act.at[k], sems.at[k]))
    for i, ref in enumerate(cots):
        first.append(pltpu.make_async_copy(ref, cot.at[pl.ds(2 * i, 2)], sems.at[8 + i]))
    for i, ref in enumerate(grads):
        rows = pl.ds((i % 2) * CUTS[0], ref.shape[0])
        later.append(pltpu.make_async_copy(ref, grad.at[i // 2, rows], sems.at[16 + i]))
    for c in first + later:
        c.start()
    train_hot = (
        lax.broadcasted_iota(jnp.int32, (TIDS, count_train), 0) == ids_ref[...]
    ).astype(jnp.float32)
    column = lax.broadcasted_iota(jnp.int32, (8 * ROWS, QIDS), 0)
    wanted = jnp.zeros((8 * ROWS, QIDS), jnp.int32)
    for k in range(8):
        one = query_ids[2 * lax.rem(z + k, 8) + core]
        wanted = jnp.where(column // ROWS == k, one, wanted)
    query_hot = (lax.broadcasted_iota(jnp.int32, (8 * ROWS, QIDS), 1) == wanted).astype(jnp.float32)
    row = lax.broadcasted_iota(jnp.int32, (count_train * ROWS, 8 * ROWS), 0)
    col = lax.broadcasted_iota(jnp.int32, (count_train * ROWS, 8 * ROWS), 1)
    same = lax.rem(row, ROWS) == lax.rem(col, ROWS)

    def slot(d):
        d = lax.rem(d + 4, 4)
        return jnp.where(d == 2, 3, jnp.where(d == 3, 2, d))

    for c in first:
        c.wait()
    for e in range(2):
        parity = core if e == 0 else 1 - core
        fisher_ref = own_fisher if e == 0 else other_fisher
        fisher = fisher_ref[layer_index[2 * z + parity]].astype(jnp.float32)
        for k in range(8):
            t = lax.rem(k + 4 * core, 8)
            dy, dx = slot(t // 2 - y), slot(lax.rem(t, 2) * 2 + parity - x)
            unit = jnp.where(core == 0, dy * 4 + dx, dx * 4 + dy)
            weighted[k] = (fisher * outer_sum(cot[unit], act[k])).astype(jnp.bfloat16)
        for c in later[2 * e : 2 * e + 2]:
            c.wait()
        total = jnp.zeros((count_train * ROWS, 8 * ROWS), jnp.float32)
        for r in range(0, HW, ROWS):
            lhs = grad[e, :, r : r + ROWS, :].reshape(count_train * ROWS, HALF)
            rhs = weighted[:, r : r + ROWS, :].reshape(8 * ROWS, HALF)
            total += lax.dot_general(
                lhs, rhs, (((1,), (1,)), ((), ())), preferred_element_type=jnp.float32
            )
        total = jnp.where(same, total, 0.0).reshape(count_train, ROWS, 8 * ROWS).sum(axis=1) * SCALE
        total = jnp.dot(
            total, query_hot, precision=lax.Precision.HIGHEST, preferred_element_type=jnp.float32
        )
        out_ref[e] = jnp.dot(
            train_hot, total, precision=lax.Precision.HIGHEST, preferred_element_type=jnp.float32
        )


def pair_scores(acts, cots, own_grads, other_grads, own_fisher, other_fisher, ids, query_ids, layers):
    count = ids.shape[0]
    bf = jnp.bfloat16
    return pl.pallas_call(
        functools.partial(pair_kernel, count),
        in_specs=[ANY] * 20 + [VMEM] * 3 + [SMEM, SMEM],
        out_specs=VMEM,
        out_shape=jax.ShapeDtypeStruct((2, TIDS, QIDS), jnp.float32),
        scratch_shapes=[
            pltpu.VMEM((16,) + cots[0].shape[1:], bf),
            pltpu.VMEM((2, count, HW, HALF), bf),
            pltpu.VMEM((8, HW, HALF), bf),
            pltpu.VMEM((8, SEQ, HALF), bf),
            pltpu.SemaphoreType.DMA((20,)),
        ],
        name="pair_scores",
        compiler_params=pltpu.CompilerParams(vmem_limit_bytes=56 * 2**20),
        cost_estimate=pl.CostEstimate(
            flops=2 * 16 * HW * HALF * SEQ * 4, bytes_accessed=20 * 2**20, transcendentals=0
        ),
    )(*acts, *cots, *own_grads, *other_grads, own_fisher, other_fisher, ids.reshape(1, count), query_ids, layers)


def offset_of(y, x):
    return (2 * y + x // 2) % 8


def local(
    train_inputs,
    train_cotangents,
    train_ids,
    query_projection_inputs,
    query_output_cotangents,
    query_ids,
    fisher_diagonal_weight,
    layer_index,
):
    core, z, y = lax.axis_index("core"), lax.axis_index("z"), lax.axis_index("y")
    x = lax.axis_index("xhi") * 2 + lax.axis_index("xlo")
    up = lambda y, x, z, c: (y, x, z + 1, c)
    down = lambda y, x, z, c: (y, x, z - 1, c)
    swap = lambda y, x, z, c: (y, x, z, 1 - c)

    def turn(k, first):
        def to(y, x, z, c):
            return (y, x - k, z, c) if (c == 0) == first else (y - k, x, z, c)

        return to

    own_x = query_projection_inputs[0]
    m1 = send(own_x, up)
    p1 = send(own_x, down)
    a = (2 * y + x // 2 + 4 * core) % 8
    head = 2 * ((z - a) % 8) + x % 2
    unit = lax.dynamic_slice_in_dim(query_output_cotangents[0], head * HW, HW, 1)
    unit = jnp.pad(unit, ((0, -SEQ % 8), (0, 0)))
    unit = send(unit, lambda y, x, z, c: (y, x, z - offset_of(y, x) - 4 * c, c))
    other_fisher = send(fisher_diagonal_weight, swap)
    own_a = train_grad(train_cotangents, train_inputs, 0, CUTS[0])
    m2 = send(m1, up)
    p2 = send(p1, down)
    parts = [unit, send(unit, turn(1, True)), send(unit, turn(-1, True)), send(unit, turn(2, True))]
    other_a = send(own_a, swap)
    own_b = train_grad(train_cotangents, train_inputs, CUTS[0], CUTS[1])
    la, lb = stack(*parts[:2]), stack(*parts[2:])
    m3 = send(m2, up)
    p3 = send(p2, down)
    lpa, lpb = send(la, turn(1, False)), send(lb, turn(1, False))
    lma, lmb = send(la, turn(-1, False)), send(lb, turn(-1, False))
    other_b = send(own_b, swap)
    far = lax.select(core == 0, m3, p3)
    f4 = send(far, lambda y, x, z, c: (y, x, z + 1 - 2 * c, c))
    l2a = send(lpa, turn(1, False))
    l2b = send(lmb, turn(-1, False))
    buckets = pair_scores(
        (own_x, p1, p2, p3, f4, m3, m2, m1),
        (la, lb, lpa, lpb, lma, lmb, l2a, l2b),
        (own_a, own_b),
        (other_a, other_b),
        fisher_diagonal_weight,
        other_fisher,
        train_ids,
        query_ids,
        layer_index,
    )
    buckets = buckets[0] + send(buckets[1], swap)
    shares = lax.all_to_all(
        buckets.reshape(NY * NXL * NXH, 4, QIDS), ("y", "xlo", "xhi"), 0, 0, tiled=True
    )
    return jnp.sum(shares, axis=0)[:, :, None]


def solution(mesh):
    fine = Mesh(mesh.devices.reshape(NY, NXL, NZ, NC, NXH), AXES)
    dp, tensor, fisher = ("y", "xlo"), ("z", "core"), "xhi"
    in_specs = (
        P(dp, None, fisher),
        P(dp, None, tensor),
        P(dp),
        P(tensor, None, fisher),
        P(tensor, None, None),
        P(),
        P(None, tensor, fisher),
        P(),
    )
    out_specs = P(("y", "xlo", "xhi"), None, tensor)
    return jax.shard_map(local, mesh=fine, in_specs=in_specs, out_specs=out_specs, check_vma=False)
```

profile of v0, /device:TPU:1, one launch (start us, length us, event | category | flops | bytes accessed | tf_op | source)
XLA Modules:
  0.0 107.9 jit_solution(10984146623546959690)
XLA Ops:
  0.0 0.0 copy-start
  0.0 5.5 %train_grad.2.refs_16_ = bf16[11,240,640]{2,1,0:T(8,128)(2,1)} custom-call(bf16[22,257,240]{2,1,0:T(8,128)(2,1)} %cot_hbm.3, bf16[22,257,640]{2,1,0:T(8,128)(2,1)} %act_hbm.3), custom_call_target="tpu_custom_call" | custom-call | flops 3473817600 | bytes 8354720 | tf_op jit(solution)/shard_map/train_grad/pallas_call | solution.py:68
  5.5 0.0 copy-start.5
  5.5 3.3 %collective-permute-start.17 = (bf16[11,240,640]{2,1,0:T(8,128)(2,1)}, bf16[11,240,640]{2,1,0:T(8,128)(2,1)}, u32[]{:S(2)}, u32[]{:S(2)}) collective-permute-start(bf16[11,240,640]{2,1,0:T(8,128)(2,1)} %train_grad.2.refs_16_), channel_id=1, source_target_pairs={{0,2},{2,0},{4,6},{6,4},{8,10},{10,8},{12,14},{14,12},{16,18},{18,... | collective-permute-start | bytes 10137608 | tf_op jit(solution)/shard_map/ppermute | solution.py:35
  8.8 5.4 %train_grad.3.refs_17_ = bf16[11,240,640]{2,1,0:T(8,128)(2,1)} custom-call(bf16[22,257,240]{2,1,0:T(8,128)(2,1)} %cot_hbm.3, bf16[22,257,640]{2,1,0:T(8,128)(2,1)} %act_hbm.3), custom_call_target="tpu_custom_call" | custom-call | flops 3473817600 | bytes 8354720 | tf_op jit(solution)/shard_map/train_grad/pallas_call | solution.py:68
  14.2 0.1 collective-permute-start.18
  14.3 0.0 copy-done
  14.4 0.1 dynamic-slice_bitcast_fusion
  14.5 7.1 %collective-permute-start.7 = (bf16[264,240]{1,0:T(8,128)(2,1)S(1)}, bf16[264,240]{1,0:T(8,128)(2,1)S(1)}, u32[]{:S(2)}, u32[]{:S(2)}) collective-permute-start(bf16[264,240]{1,0:T(8,128)(2,1)S(1)} %pad.4), channel_id=1, source_target_pairs={{0,0},{2,18},{4,4},{6,22},{8,8},{10,26},{12,12},{14,30},{16,16},{1... | collective-permute-start | bytes 380168 | tf_op jit(solution)/shard_map/ppermute | solution.py:35
  21.6 2.6 %collective-permute-done.7.refs_0_ = bf16[264,240]{1,0:T(8,128)(2,1)S(1)} collective-permute-done((bf16[264,240]{1,0:T(8,128)(2,1)S(1)}, bf16[264,240]{1,0:T(8,128)(2,1)S(1)}, u32[]{:S(2)}, u32[]{:S(2)}) %collective-permute-start.7) | collective-permute-done | bytes 126752 | tf_op jit(solution)/shard_map/ppermute | solution.py:35
  24.3 0.0 collective-permute-start.10
  24.3 2.6 %collective-permute-start.8 = (bf16[264,240]{1,0:T(8,128)(2,1)S(1)}, bf16[264,240]{1,0:T(8,128)(2,1)S(1)}, u32[]{:S(2)}, u32[]{:S(2)}) collective-permute-start(bf16[264,240]{1,0:T(8,128)(2,1)S(1)} %collective-permute-done.7.refs_0_), channel_id=1, source_target_pairs={{0,33},{2,194},{4,37},{6,198},{8,41},{10,202},{12,45},{14,206},{16... | collective-permute-start | bytes 380168 | tf_op jit(solution)/shard_map/ppermute | solution.py:35
  26.9 0.0 copy-done.5
  26.9 2.1 %collective-permute-start.3 = (bf16[257,640]{1,0:T(8,128)(2,1)S(1)}, bf16[257,640]{1,0:T(8,128)(2,1)S(1)}, u32[]{:S(2)}, u32[]{:S(2)}) collective-permute-start(bf16[257,640]{1,0:T(8,128)(2,1)S(1)} %bitcast.15), channel_id=1, source_target_pairs={{0,4},{2,6},{4,8},{6,10},{8,12},{10,14},{12,16},{14,18},{16,20},{1... | collective-permute-start | bytes 986888 | tf_op jit(solution)/shard_map/ppermute | solution.py:35
  29.0 0.6 collective-permute-done.10.refs_1_
  29.6 4.1 %collective-permute-start = (bf16[257,640]{1,0:T(8,128)(2,1)S(1)}, bf16[257,640]{1,0:T(8,128)(2,1)S(1)}, u32[]{:S(2)}, u32[]{:S(2)}) collective-permute-start(bf16[257,640]{1,0:T(8,128)(2,1)S(1)} %bitcast.16), channel_id=1, source_target_pairs={{0,28},{2,30},{4,0},{6,2},{8,4},{10,6},{12,8},{14,10},{16,12},{18,... | collective-permute-start | bytes 986888 | tf_op jit(solution)/shard_map/ppermute | solution.py:35
  33.8 0.0 collective-permute-done.8.refs_1_
  33.8 0.0 collective-permute-start.9
  33.8 0.0 copy-start.1
  33.8 5.3 %collective-permute-done.9.refs_0_ = bf16[264,240]{1,0:T(8,128)(2,1)S(1)} collective-permute-done((bf16[264,240]{1,0:T(8,128)(2,1)S(1)}, bf16[264,240]{1,0:T(8,128)(2,1)S(1)}, u32[]{:S(2)}, u32[]{:S(2)}) %collective-permute-start.9) | collective-permute-done | bytes 126752 | tf_op jit(solution)/shard_map/ppermute | solution.py:35
  39.1 1.0 collective-permute-start.13
  40.2 0.0 collective-permute-done.3.refs_7_
  40.2 0.0 collective-permute-start.4
  40.2 1.0 collective-permute-done.refs_1_
  41.1 3.1 %collective-permute-start.1 = (bf16[257,640]{1,0:T(8,128)(2,1)S(1)}, bf16[257,640]{1,0:T(8,128)(2,1)}, u32[]{:S(2)}, u32[]{:S(2)}) collective-permute-start(bf16[257,640]{1,0:T(8,128)(2,1)S(1)} %collective-permute-done.refs_1_), channel_id=1, source_target_pairs={{0,28},{2,30},{4,0},{6,2},{8,4},{10,6},{12,8},{14,10},{16,12},{18,... | collective-permute-start | bytes 986888 | tf_op jit(solution)/shard_map/ppermute | solution.py:35
  44.3 1.7 %collective-permute-done.13.refs_12_ = bf16[2,264,240]{2,1,0:T(8,128)(2,1)S(1)} collective-permute-done((bf16[2,264,240]{2,1,0:T(8,128)(2,1)S(1)}, bf16[2,264,240]{2,1,0:T(8,128)(2,1)S(1)}, u32[]{:S(2)}, u32[]{:S(2)}) %collective-permute-start.13) | collective-permute-done | bytes 253472 | tf_op jit(solution)/shard_map/ppermute | solution.py:35
  46.0 0.7 collective-permute-start.11
  46.7 1.0 collective-permute-done.4.refs_6_
  47.7 0.0 collective-permute-start.5
  47.7 1.2 %collective-permute-done.1.refs_2_ = bf16[257,640]{1,0:T(8,128)(2,1)} collective-permute-done((bf16[257,640]{1,0:T(8,128)(2,1)S(1)}, bf16[257,640]{1,0:T(8,128)(2,1)}, u32[]{:S(2)}, u32[]{:S(2)}) %collective-permute-start.1) | collective-permute-done | bytes 328992 | tf_op jit(solution)/shard_map/ppermute | solution.py:35
  48.9 3.5 %collective-permute-start.2 = (bf16[257,640]{1,0:T(8,128)(2,1)}, bf16[257,640]{1,0:T(8,128)(2,1)S(1)}, u32[]{:S(2)}, u32[]{:S(2)}) collective-permute-start(bf16[257,640]{1,0:T(8,128)(2,1)} %collective-permute-done.1.refs_2_), channel_id=1, source_target_pairs={{0,28},{2,30},{4,0},{6,2},{8,4},{10,6},{12,8},{14,10},{16,12},{18,... | collective-permute-start | bytes 986888 | tf_op jit(solution)/shard_map/ppermute | solution.py:35
  52.5 0.0 collective-permute-done.11.refs_10_
  52.5 0.7 copy-done.11
  53.2 3.9 %collective-permute-start.19 = (bf16[2,240,640]{2,1,0:T(8,128)(2,1)}, bf16[2,240,640]{2,1,0:T(8,128)(2,1)}, u32[]{:S(2)}, u32[]{:S(2)}) collective-permute-start(bf16[2,240,640]{2,1,0:T(8,128)(2,1)} %refs_20_.1), channel_id=1, source_target_pairs={{0,2},{2,0},{4,6},{6,4},{8,10},{10,8},{12,14},{14,12},{16,18},{18,... | collective-permute-start | bytes 1843208 | tf_op jit(solution)/shard_map/ppermute | solution.py:35
  57.1 0.0 copy-start.2
  57.1 0.0 collective-permute-done.5.refs_5_
  57.1 0.0 copy-done.6
  57.1 0.0 copy-done.7
  57.1 0.0 copy-done.8
  57.1 0.0 copy-start.3
  57.1 0.2 collective-permute-start.14
  57.4 0.0 collective-permute-done.2.refs_3_
  57.4 2.8 %collective-permute-start.12 = (bf16[2,264,240]{2,1,0:T(8,128)(2,1)S(1)}, bf16[2,264,240]{2,1,0:T(8,128)(2,1)S(1)}, u32[]{:S(2)}, u32[]{:S(2)}) collective-permute-start(bf16[2,264,240]{2,1,0:T(8,128)(2,1)S(1)} %stack.3.refs_9_), channel_id=1, source_target_pairs={{0,192},{2,35},{4,196},{6,39},{8,200},{10,43},{12,204},{14,47},{16... | collective-permute-start | bytes 760328 | tf_op jit(solution)/shard_map/ppermute | solution.py:35
  60.2 3.8 %collective-permute-done.14.refs_13_ = bf16[2,264,240]{2,1,0:T(8,128)(2,1)} collective-permute-done((bf16[2,264,240]{2,1,0:T(8,128)(2,1)S(1)}, bf16[2,264,240]{2,1,0:T(8,128)(2,1)}, u32[]{:S(2)}, u32[]{:S(2)}) %collective-permute-start.14) | collective-permute-done | bytes 253472 | tf_op jit(solution)/shard_map/ppermute | solution.py:35
  64.0 2.0 %collective-permute-start.6 = (bf16[257,640]{1,0:T(8,128)(2,1)S(1)}, bf16[257,640]{1,0:T(8,128)(2,1)S(1)}, u32[]{:S(2)}, u32[]{:S(2)}) collective-permute-start(bf16[257,640]{1,0:T(8,128)(2,1)S(1)} %broadcast_select_fusion), channel_id=1, source_target_pairs={{0,4},{2,30},{4,8},{6,2},{8,12},{10,6},{12,16},{14,10},{16,20},{18... | collective-permute-start | bytes 986888 | tf_op jit(solution)/shard_map/ppermute | solution.py:35
  66.0 0.0 collective-permute-done.12.refs_11_
  66.0 1.4 %collective-permute-start.15 = (bf16[2,264,240]{2,1,0:T(8,128)(2,1)}, bf16[2,264,240]{2,1,0:T(8,128)(2,1)S(1)}, u32[]{:S(2)}, u32[]{:S(2)}) collective-permute-start(bf16[2,264,240]{2,1,0:T(8,128)(2,1)} %copy-done.11), channel_id=1, source_target_pairs={{0,192},{2,35},{4,196},{6,39},{8,200},{10,43},{12,204},{14,47},{16... | collective-permute-start | bytes 760328 | tf_op jit(solution)/shard_map/ppermute | solution.py:35
  67.5 0.0 collective-permute-done.19.refs_21_
  67.5 0.0 collective-permute-start.16
  67.5 4.3 %collective-permute-done.15.refs_14_ = bf16[2,264,240]{2,1,0:T(8,128)(2,1)S(1)} collective-permute-done((bf16[2,264,240]{2,1,0:T(8,128)(2,1)}, bf16[2,264,240]{2,1,0:T(8,128)(2,1)S(1)}, u32[]{:S(2)}, u32[]{:S(2)}) %collective-permute-start.15) | collective-permute-done | bytes 253472 | tf_op jit(solution)/shard_map/ppermute | solution.py:35
  71.8 2.4 %collective-permute-done.16.refs_15_ = bf16[2,264,240]{2,1,0:T(8,128)(2,1)S(1)} collective-permute-done((bf16[2,264,240]{2,1,0:T(8,128)(2,1)}, bf16[2,264,240]{2,1,0:T(8,128)(2,1)S(1)}, u32[]{:S(2)}, u32[]{:S(2)}) %collective-permute-start.16) | collective-permute-done | bytes 253472 | tf_op jit(solution)/shard_map/ppermute | solution.py:35
  74.2 0.0 collective-permute-done.6.refs_4_
  74.2 0.0 collective-permute-done.17.refs_18_
  74.2 0.0 collective-permute-done.18.refs_19_
  74.2 0.0 copy-done.1
  74.3 0.6 copy-done.14
  74.9 0.1 copy-done.9
  75.0 12.2 %pair_scores.1 = f32[2,64,16]{2,1,0:T(8,128)} custom-call(bf16[257,640]{1,0:T(8,128)(2,1)} %bitcast.14, bf16[257,640]{1,0:T(8,128)(2,1)} %copy-done.7, bf16[257,640]{1,0:T(8,128)(2,1)} %collective-permute-done.1.refs_2_, bf16[257,640]{1,0:T(8,128)(2,1)} %copy-done.4, bf16[257,640]{1,0:T(8,128)(2,1)} %copy-done.9, bf16[257,640]{1,0:T(8,128)(2,1)} %copy-done.3, ...), custom_call_target="tpu_custom_call" | custom-call | flops 5052825600 | bytes 20971520 | tf_op jit(solution)/shard_map/pair_scores/pallas_call | solution.py:172
  87.2 0.8 slice_bitcast_fusion
  88.0 8.5 %collective-permute-start.20 = (f32[64,16]{1,0:T(8,128)S(1)}, f32[64,16]{1,0:T(8,128)S(1)}, u32[]{:S(2)}, u32[]{:S(2)}) collective-permute-start(f32[64,16]{1,0:T(8,128)S(1)} %slice_bitcast_fusion), channel_id=1, source_target_pairs={{0,2},{2,0},{4,6},{6,4},{8,10},{10,8},{12,14},{14,12},{16,18},{18,... | collective-permute-start | bytes 12296 | tf_op jit(solution)/shard_map/ppermute | solution.py:35
  96.5 0.9 collective-permute-done.20
  97.4 0.8 fusion
  98.1 9.2 %all_to_all.5 = f32[16,4,16]{2,1,0:T(4,128)S(1)} all-to-all(f32[16,4,16]{2,1,0:T(4,128)S(1)} %bitcast.17), channel_id=1, replica_groups=mesh['y'=4,'xlo'=2,'z'=8,'core'=2,'xhi'=2] {'y','xlo','xhi'}, dimensions={0} | all-to-all | bytes 8192 | tf_op jit(solution)/shard_map/all_to_all | solution.py:255
  107.3 0.6 reduce_sum.9
  (20 shorter events, 0.1 us)
Async XLA Ops:
  0.0 14.3 %copy-start = (bf16[1,257,3840]{2,1,0:T(8,128)(2,1)S(1)}, bf16[1,257,3840]{2,1,0:T(8,128)(2,1)}, u32[]{:S(2)}) copy-start(bf16[1,257,3840]{2,1,0:T(8,128)(2,1)} %param.12) | copy-start | bytes 5921284
  5.5 21.4 %copy-start.5 = (bf16[1,257,640]{2,1,0:T(8,128)(2,1)S(1)}, bf16[1,257,640]{2,1,0:T(8,128)(2,1)}, u32[]{:S(2)}) copy-start(bf16[1,257,640]{2,1,0:T(8,128)(2,1)} %param.11) | copy-start | bytes 986884
  5.5 68.7 %collective-permute-start.17 = (bf16[11,240,640]{2,1,0:T(8,128)(2,1)}, bf16[11,240,640]{2,1,0:T(8,128)(2,1)}, u32[]{:S(2)}, u32[]{:S(2)}) collective-permute-start(bf16[11,240,640]{2,1,0:T(8,128)(2,1)} %train_grad.2.refs_16_), channel_id=1, source_target_pairs={{0,2},{2,0},{4,6},{6,4},{8,10},{10,8},{12,14},{14,12},{16,18},{18,... | collective-permute-start | bytes 10137608 | tf_op jit(solution)/shard_map/ppermute | solution.py:35
  14.2 60.0 %collective-permute-start.18 = (bf16[11,240,640]{2,1,0:T(8,128)(2,1)}, bf16[11,240,640]{2,1,0:T(8,128)(2,1)}, u32[]{:S(2)}, u32[]{:S(2)}) collective-permute-start(bf16[11,240,640]{2,1,0:T(8,128)(2,1)} %train_grad.3.refs_17_), channel_id=1, source_target_pairs={{0,2},{2,0},{4,6},{6,4},{8,10},{10,8},{12,14},{14,12},{16,18},{18,... | collective-permute-start | bytes 10137608 | tf_op jit(solution)/shard_map/ppermute | solution.py:35
  14.5 9.8 %collective-permute-start.7 = (bf16[264,240]{1,0:T(8,128)(2,1)S(1)}, bf16[264,240]{1,0:T(8,128)(2,1)S(1)}, u32[]{:S(2)}, u32[]{:S(2)}) collective-permute-start(bf16[264,240]{1,0:T(8,128)(2,1)S(1)} %pad.4), channel_id=1, source_target_pairs={{0,0},{2,18},{4,4},{6,22},{8,8},{10,26},{12,12},{14,30},{16,16},{1... | collective-permute-start | bytes 380168 | tf_op jit(solution)/shard_map/ppermute | solution.py:35
  24.3 5.4 %collective-permute-start.10 = (bf16[264,240]{1,0:T(8,128)(2,1)S(1)}, bf16[264,240]{1,0:T(8,128)(2,1)S(1)}, u32[]{:S(2)}, u32[]{:S(2)}) collective-permute-start(bf16[264,240]{1,0:T(8,128)(2,1)S(1)} %collective-permute-done.7.refs_0_), channel_id=1, source_target_pairs={{0,1},{2,130},{4,5},{6,134},{8,9},{10,138},{12,13},{14,142},{16,17... | collective-permute-start | bytes 380168 | tf_op jit(solution)/shard_map/ppermute | solution.py:35
  24.3 9.5 %collective-permute-start.8 = (bf16[264,240]{1,0:T(8,128)(2,1)S(1)}, bf16[264,240]{1,0:T(8,128)(2,1)S(1)}, u32[]{:S(2)}, u32[]{:S(2)}) collective-permute-start(bf16[264,240]{1,0:T(8,128)(2,1)S(1)} %collective-permute-done.7.refs_0_), channel_id=1, source_target_pairs={{0,33},{2,194},{4,37},{6,198},{8,41},{10,202},{12,45},{14,206},{16... | collective-permute-start | bytes 380168 | tf_op jit(solution)/shard_map/ppermute | solution.py:35
  26.9 13.3 %collective-permute-start.3 = (bf16[257,640]{1,0:T(8,128)(2,1)S(1)}, bf16[257,640]{1,0:T(8,128)(2,1)S(1)}, u32[]{:S(2)}, u32[]{:S(2)}) collective-permute-start(bf16[257,640]{1,0:T(8,128)(2,1)S(1)} %bitcast.15), channel_id=1, source_target_pairs={{0,4},{2,6},{4,8},{6,10},{8,12},{10,14},{12,16},{14,18},{16,20},{1... | collective-permute-start | bytes 986888 | tf_op jit(solution)/shard_map/ppermute | solution.py:35
  29.6 11.5 %collective-permute-start = (bf16[257,640]{1,0:T(8,128)(2,1)S(1)}, bf16[257,640]{1,0:T(8,128)(2,1)S(1)}, u32[]{:S(2)}, u32[]{:S(2)}) collective-permute-start(bf16[257,640]{1,0:T(8,128)(2,1)S(1)} %bitcast.16), channel_id=1, source_target_pairs={{0,28},{2,30},{4,0},{6,2},{8,4},{10,6},{12,8},{14,10},{16,12},{18,... | collective-permute-start | bytes 986888 | tf_op jit(solution)/shard_map/ppermute | solution.py:35
  33.8 5.4 %collective-permute-start.9 = (bf16[264,240]{1,0:T(8,128)(2,1)S(1)}, bf16[264,240]{1,0:T(8,128)(2,1)S(1)}, u32[]{:S(2)}, u32[]{:S(2)}) collective-permute-start(bf16[264,240]{1,0:T(8,128)(2,1)S(1)} %collective-permute-done.7.refs_0_), channel_id=1, source_target_pairs={{0,32},{2,66},{4,36},{6,70},{8,40},{10,74},{12,44},{14,78},{16,48}... | collective-permute-start | bytes 380168 | tf_op jit(solution)/shard_map/ppermute | solution.py:35
  33.8 40.4 %copy-start.1 = (bf16[2,264,240]{2,1,0:T(8,128)(2,1)}, bf16[2,264,240]{2,1,0:T(8,128)(2,1)S(1)}, u32[]{:S(2)}) copy-start(bf16[2,264,240]{2,1,0:T(8,128)(2,1)S(1)} %stack.2.refs_8_) | copy-start | bytes 760324
  39.1 6.8 %collective-permute-start.13 = (bf16[2,264,240]{2,1,0:T(8,128)(2,1)S(1)}, bf16[2,264,240]{2,1,0:T(8,128)(2,1)S(1)}, u32[]{:S(2)}, u32[]{:S(2)}) collective-permute-start(bf16[2,264,240]{2,1,0:T(8,128)(2,1)S(1)} %stack.2.refs_8_), channel_id=1, source_target_pairs={{0,64},{2,34},{4,68},{6,38},{8,72},{10,42},{12,76},{14,46},{16,80}... | collective-permute-start | bytes 760328 | tf_op jit(solution)/shard_map/ppermute | solution.py:35
  40.2 16.9 %copy-start.6 = (bf16[257,640]{1,0:T(8,128)(2,1)}, bf16[257,640]{1,0:T(8,128)(2,1)S(1)}, u32[]{:S(2)}) copy-start(bf16[257,640]{1,0:T(8,128)(2,1)S(1)} %collective-permute-done.3.refs_7_) | copy-start | bytes 986884
  40.2 7.5 %collective-permute-start.4 = (bf16[257,640]{1,0:T(8,128)(2,1)S(1)}, bf16[257,640]{1,0:T(8,128)(2,1)S(1)}, u32[]{:S(2)}, u32[]{:S(2)}) collective-permute-start(bf16[257,640]{1,0:T(8,128)(2,1)S(1)} %collective-permute-done.3.refs_7_), channel_id=1, source_target_pairs={{0,4},{2,6},{4,8},{6,10},{8,12},{10,14},{12,16},{14,18},{16,20},{1... | collective-permute-start | bytes 986888 | tf_op jit(solution)/shard_map/ppermute | solution.py:35
  41.1 16.0 %copy-start.7 = (bf16[257,640]{1,0:T(8,128)(2,1)}, bf16[257,640]{1,0:T(8,128)(2,1)S(1)}, u32[]{:S(2)}) copy-start(bf16[257,640]{1,0:T(8,128)(2,1)S(1)} %collective-permute-done.refs_1_) | copy-start | bytes 986884
  41.1 7.8 %collective-permute-start.1 = (bf16[257,640]{1,0:T(8,128)(2,1)S(1)}, bf16[257,640]{1,0:T(8,128)(2,1)}, u32[]{:S(2)}, u32[]{:S(2)}) collective-permute-start(bf16[257,640]{1,0:T(8,128)(2,1)S(1)} %collective-permute-done.refs_1_), channel_id=1, source_target_pairs={{0,28},{2,30},{4,0},{6,2},{8,4},{10,6},{12,8},{14,10},{16,12},{18,... | collective-permute-start | bytes 986888 | tf_op jit(solution)/shard_map/ppermute | solution.py:35
  46.0 28.3 %copy-start.10 = (bf16[2,264,240]{2,1,0:T(8,128)(2,1)}, bf16[2,264,240]{2,1,0:T(8,128)(2,1)S(1)}, u32[]{:S(2)}) copy-start(bf16[2,264,240]{2,1,0:T(8,128)(2,1)S(1)} %collective-permute-done.13.refs_12_) | copy-start | bytes 760324
  46.0 6.5 %collective-permute-start.11 = (bf16[2,264,240]{2,1,0:T(8,128)(2,1)S(1)}, bf16[2,264,240]{2,1,0:T(8,128)(2,1)S(1)}, u32[]{:S(2)}, u32[]{:S(2)}) collective-permute-start(bf16[2,264,240]{2,1,0:T(8,128)(2,1)S(1)} %stack.2.refs_8_), channel_id=1, source_target_pairs={{0,192},{2,35},{4,196},{6,39},{8,200},{10,43},{12,204},{14,47},{16... | collective-permute-start | bytes 760328 | tf_op jit(solution)/shard_map/ppermute | solution.py:35
  47.7 9.4 %copy-start.8 = (bf16[257,640]{1,0:T(8,128)(2,1)}, bf16[257,640]{1,0:T(8,128)(2,1)S(1)}, u32[]{:S(2)}) copy-start(bf16[257,640]{1,0:T(8,128)(2,1)S(1)} %collective-permute-done.4.refs_6_) | copy-start | bytes 986884
  47.7 9.4 %collective-permute-start.5 = (bf16[257,640]{1,0:T(8,128)(2,1)S(1)}, bf16[257,640]{1,0:T(8,128)(2,1)S(1)}, u32[]{:S(2)}, u32[]{:S(2)}) collective-permute-start(bf16[257,640]{1,0:T(8,128)(2,1)S(1)} %collective-permute-done.4.refs_6_), channel_id=1, source_target_pairs={{0,4},{2,6},{4,8},{6,10},{8,12},{10,14},{12,16},{14,18},{16,20},{1... | collective-permute-start | bytes 986888 | tf_op jit(solution)/shard_map/ppermute | solution.py:35
  48.9 8.5 %collective-permute-start.2 = (bf16[257,640]{1,0:T(8,128)(2,1)}, bf16[257,640]{1,0:T(8,128)(2,1)S(1)}, u32[]{:S(2)}, u32[]{:S(2)}) collective-permute-start(bf16[257,640]{1,0:T(8,128)(2,1)} %collective-permute-done.1.refs_2_), channel_id=1, source_target_pairs={{0,28},{2,30},{4,0},{6,2},{8,4},{10,6},{12,8},{14,10},{16,12},{18,... | collective-permute-start | bytes 986888 | tf_op jit(solution)/shard_map/ppermute | solution.py:35
  52.5 0.7 copy-start.11
  53.2 14.3 %collective-permute-start.19 = (bf16[2,240,640]{2,1,0:T(8,128)(2,1)}, bf16[2,240,640]{2,1,0:T(8,128)(2,1)}, u32[]{:S(2)}, u32[]{:S(2)}) collective-permute-start(bf16[2,240,640]{2,1,0:T(8,128)(2,1)} %refs_20_.1), channel_id=1, source_target_pairs={{0,2},{2,0},{4,6},{6,4},{8,10},{10,8},{12,14},{14,12},{16,18},{18,... | collective-permute-start | bytes 1843208 | tf_op jit(solution)/shard_map/ppermute | solution.py:35
  57.1 17.1 %copy-start.2 = (bf16[2,264,240]{2,1,0:T(8,128)(2,1)}, bf16[2,264,240]{2,1,0:T(8,128)(2,1)S(1)}, u32[]{:S(2)}) copy-start(bf16[2,264,240]{2,1,0:T(8,128)(2,1)S(1)} %stack.3.refs_9_) | copy-start | bytes 760324
  57.1 17.1 %copy-start.3 = (bf16[257,640]{1,0:T(8,128)(2,1)}, bf16[257,640]{1,0:T(8,128)(2,1)S(1)}, u32[]{:S(2)}) copy-start(bf16[257,640]{1,0:T(8,128)(2,1)S(1)} %collective-permute-done.5.refs_5_) | copy-start | bytes 986884
  57.1 6.9 %collective-permute-start.14 = (bf16[2,264,240]{2,1,0:T(8,128)(2,1)S(1)}, bf16[2,264,240]{2,1,0:T(8,128)(2,1)}, u32[]{:S(2)}, u32[]{:S(2)}) collective-permute-start(bf16[2,264,240]{2,1,0:T(8,128)(2,1)S(1)} %stack.3.refs_9_), channel_id=1, source_target_pairs={{0,64},{2,34},{4,68},{6,38},{8,72},{10,42},{12,76},{14,46},{16,80}... | collective-permute-start | bytes 760328 | tf_op jit(solution)/shard_map/ppermute | solution.py:35
  57.4 16.9 %copy-start.4 = (bf16[257,640]{1,0:T(8,128)(2,1)}, bf16[257,640]{1,0:T(8,128)(2,1)S(1)}, u32[]{:S(2)}) copy-start(bf16[257,640]{1,0:T(8,128)(2,1)S(1)} %collective-permute-done.2.refs_3_) | copy-start | bytes 986884
  57.4 8.6 %collective-permute-start.12 = (bf16[2,264,240]{2,1,0:T(8,128)(2,1)S(1)}, bf16[2,264,240]{2,1,0:T(8,128)(2,1)S(1)}, u32[]{:S(2)}, u32[]{:S(2)}) collective-permute-start(bf16[2,264,240]{2,1,0:T(8,128)(2,1)S(1)} %stack.3.refs_9_), channel_id=1, source_target_pairs={{0,192},{2,35},{4,196},{6,39},{8,200},{10,43},{12,204},{14,47},{16... | collective-permute-start | bytes 760328 | tf_op jit(solution)/shard_map/ppermute | solution.py:35
  64.0 10.2 %collective-permute-start.6 = (bf16[257,640]{1,0:T(8,128)(2,1)S(1)}, bf16[257,640]{1,0:T(8,128)(2,1)S(1)}, u32[]{:S(2)}, u32[]{:S(2)}) collective-permute-start(bf16[257,640]{1,0:T(8,128)(2,1)S(1)} %broadcast_select_fusion), channel_id=1, source_target_pairs={{0,4},{2,30},{4,8},{6,2},{8,12},{10,6},{12,16},{14,10},{16,20},{18... | collective-permute-start | bytes 986888 | tf_op jit(solution)/shard_map/ppermute | solution.py:35
  66.0 8.3 %copy-start.12 = (bf16[2,264,240]{2,1,0:T(8,128)(2,1)}, bf16[2,264,240]{2,1,0:T(8,128)(2,1)S(1)}, u32[]{:S(2)}) copy-start(bf16[2,264,240]{2,1,0:T(8,128)(2,1)S(1)} %collective-permute-done.12.refs_11_) | copy-start | bytes 760324
  66.0 5.8 %collective-permute-start.15 = (bf16[2,264,240]{2,1,0:T(8,128)(2,1)}, bf16[2,264,240]{2,1,0:T(8,128)(2,1)S(1)}, u32[]{:S(2)}, u32[]{:S(2)}) collective-permute-start(bf16[2,264,240]{2,1,0:T(8,128)(2,1)} %copy-done.11), channel_id=1, source_target_pairs={{0,192},{2,35},{4,196},{6,39},{8,200},{10,43},{12,204},{14,47},{16... | collective-permute-start | bytes 760328 | tf_op jit(solution)/shard_map/ppermute | solution.py:35
  67.5 6.7 %collective-permute-start.16 = (bf16[2,264,240]{2,1,0:T(8,128)(2,1)}, bf16[2,264,240]{2,1,0:T(8,128)(2,1)S(1)}, u32[]{:S(2)}, u32[]{:S(2)}) collective-permute-start(bf16[2,264,240]{2,1,0:T(8,128)(2,1)} %collective-permute-done.14.refs_13_), channel_id=1, source_target_pairs={{0,64},{2,34},{4,68},{6,38},{8,72},{10,42},{12,76},{14,46},{16,80}... | collective-permute-start | bytes 760328 | tf_op jit(solution)/shard_map/ppermute | solution.py:35
  71.8 2.5 %copy-start.13 = (bf16[2,264,240]{2,1,0:T(8,128)(2,1)}, bf16[2,264,240]{2,1,0:T(8,128)(2,1)S(1)}, u32[]{:S(2)}) copy-start(bf16[2,264,240]{2,1,0:T(8,128)(2,1)S(1)} %collective-permute-done.15.refs_14_) | copy-start | bytes 760324
  74.2 0.7 copy-start.14
  74.2 0.8 copy-start.9
  88.0 9.4 %collective-permute-start.20 = (f32[64,16]{1,0:T(8,128)S(1)}, f32[64,16]{1,0:T(8,128)S(1)}, u32[]{:S(2)}, u32[]{:S(2)}) collective-permute-start(f32[64,16]{1,0:T(8,128)S(1)} %slice_bitcast_fusion), channel_id=1, source_target_pairs={{0,2},{2,0},{4,6},{6,4},{8,10},{10,8},{12,14},{14,12},{16,18},{18,... | collective-permute-start | bytes 12296 | tf_op jit(solution)/shard_map/ppermute | solution.py:35
where the time goes:
time: 108 us
  starting transfers between devices  46.7 us (43%)
  waiting for transfers between devices  24.9 us (23%)
  Pallas kernels  23.1 us (21%)
  blocking collectives  9.18 us (8%)
  local copies, waits for them, and re-layouts  2.4 us (2%)
  other arithmetic  1.41 us (1%)
    ppermute x21, starting transfers between devices, send(): lax.ppermute(value, AXES, [(flat(*p), flat(*to(*p))) for p in places])  46.7 us
    ppermute x21, waiting for transfers between devices, send(): lax.ppermute(value, AXES, [(flat(*p), flat(*to(*p))) for p in places])  24.9 us
    pallas_call x1, Pallas kernels, pair_scores(): pl.pallas_call(functools.partial(pair_kernel, count), in_specs=[ANY] * 20...  12.2 us
    pallas_call x2, Pallas kernels, train_grad(): pl.pallas_call(functools.partial(train_kernel, first, group), in_specs=[A...  10.9 us
    all_to_all x1, blocking collectives, local(): lax.all_to_all(buckets.reshape(NY * NXL * NXH, 4, QIDS), ('y', 'xlo', 'xh...  9.18 us
  transfers between devices with their start and end apart: 21, of which 11 were waited for; matrix products, arithmetic and copies ran while one was open for 0% of the time, Pallas kernels for 5%

commit v1 on v0

--- a/solution.py
+++ b/solution.py
@@ -17,9 +17,9 @@
 HW = 3 * HEAD_DIM
 HALF = D // 2
 ROWS = 16
+CUTS = (11, 11)
 NY, NXL, NZ, NC, NXH = 4, 2, 8, 2, 2
 AXES = ("y", "xlo", "z", "core", "xhi")
-CUTS = (11, 11)
 SCALE = 1.0 / (SEQ * math.sqrt(HW * D))
 ANY = pl.BlockSpec(memory_space=pl.ANY)
 VMEM = pl.BlockSpec(memory_space=pltpu.VMEM)
@@ -85,6 +85,31 @@
     )(cot, act)
 
 
+def turned_sum(turned, act):
+    body = lax.dot_general(
+        turned[:HW], act[:BODY], (((1,), (0,)), ((), ())), preferred_element_type=jnp.float32
+    )
+    column = jnp.transpose(turned[HW : HW + 1].astype(jnp.float32))[:HW]
+    return body + column * act[BODY:SEQ].astype(jnp.float32)
+
+
+def pack_kernel(cot_ref, out_ref):
+    out_ref[:HW] = jnp.transpose(cot_ref[:BODY])
+    last = jnp.broadcast_to(cot_ref[BODY:SEQ], (8, HW))
+    out_ref[HW:] = jnp.concatenate([last, jnp.zeros((8, BODY - HW), last.dtype)], axis=1)
+
+
+def pack(cot):
+    return pl.pallas_call(
+        pack_kernel,
+        in_specs=[VMEM],
+        out_specs=VMEM,
+        out_shape=jax.ShapeDtypeStruct((HW + 8, BODY), cot.dtype),
+        name="pack",
+        compiler_params=pltpu.CompilerParams(vmem_limit_bytes=4 * 2**20),
+    )(cot)
+
+
 def stack_kernel(*refs):
     *sources, out = refs
     for i, ref in enumerate(sources):
@@ -107,17 +132,21 @@
     cots, refs = refs[:8], refs[8:]
     grads, refs = refs[:4], refs[4:]
     own_fisher, other_fisher, ids_ref, query_ids, layer_index, out_ref = refs[:6]
-    cot, grad, weighted, act, sems = refs[6:]
+    cot, grad, weighted, act, chosen, sems = refs[6:]
     core, z, y = lax.axis_index("core"), lax.axis_index("z"), lax.axis_index("y")
     x = lax.axis_index("xhi") * 2 + lax.axis_index("xlo")
-    first, later = [], []
+    first = []
     for k, ref in enumerate(acts):
         first.append(pltpu.make_async_copy(ref, act.at[k], sems.at[k]))
     for i, ref in enumerate(cots):
         first.append(pltpu.make_async_copy(ref, cot.at[pl.ds(2 * i, 2)], sems.at[8 + i]))
+    for e, ref in enumerate((own_fisher, other_fisher)):
+        layer = layer_index[2 * z + (core if e == 0 else 1 - core)]
+        first.append(pltpu.make_async_copy(ref.at[layer], chosen.at[e], sems.at[16 + e]))
+    later = []
     for i, ref in enumerate(grads):
-        rows = pl.ds((i % 2) * CUTS[0], ref.shape[0])
-        later.append(pltpu.make_async_copy(ref, grad.at[i // 2, rows], sems.at[16 + i]))
+        e, rows = i // 2, pl.ds((i % 2) * CUTS[0], ref.shape[0])
+        later.append(pltpu.make_async_copy(ref, grad.at[e, rows], sems.at[18 + i]))
     for c in first + later:
         c.start()
     train_hot = (
@@ -141,13 +170,12 @@
         c.wait()
     for e in range(2):
         parity = core if e == 0 else 1 - core
-        fisher_ref = own_fisher if e == 0 else other_fisher
-        fisher = fisher_ref[layer_index[2 * z + parity]].astype(jnp.float32)
+        fisher = chosen[e].astype(jnp.float32)
         for k in range(8):
             t = lax.rem(k + 4 * core, 8)
             dy, dx = slot(t // 2 - y), slot(lax.rem(t, 2) * 2 + parity - x)
             unit = jnp.where(core == 0, dy * 4 + dx, dx * 4 + dy)
-            weighted[k] = (fisher * outer_sum(cot[unit], act[k])).astype(jnp.bfloat16)
+            weighted[k] = (fisher * turned_sum(cot[unit], act[k])).astype(jnp.bfloat16)
         for c in later[2 * e : 2 * e + 2]:
             c.wait()
         total = jnp.zeros((count_train * ROWS, 8 * ROWS), jnp.float32)
@@ -161,32 +189,35 @@
         total = jnp.dot(
             total, query_hot, precision=lax.Precision.HIGHEST, preferred_element_type=jnp.float32
         )
-        out_ref[e] = jnp.dot(
+        total = jnp.dot(
             train_hot, total, precision=lax.Precision.HIGHEST, preferred_element_type=jnp.float32
         )
-
-
-def pair_scores(acts, cots, own_grads, other_grads, own_fisher, other_fisher, ids, query_ids, layers):
+        for i in range(TIDS // 4):
+            out_ref[2 * i + parity] = total[4 * i : 4 * i + 4]
+
+
+def pair_scores(acts, cots, grads, own_fisher, other_fisher, ids, query_ids, layers):
     count = ids.shape[0]
     bf = jnp.bfloat16
     return pl.pallas_call(
         functools.partial(pair_kernel, count),
-        in_specs=[ANY] * 20 + [VMEM] * 3 + [SMEM, SMEM],
+        in_specs=[ANY] * 22 + [VMEM, SMEM, SMEM],
         out_specs=VMEM,
-        out_shape=jax.ShapeDtypeStruct((2, TIDS, QIDS), jnp.float32),
+        out_shape=jax.ShapeDtypeStruct((TIDS // 2, 4, QIDS), jnp.float32),
         scratch_shapes=[
             pltpu.VMEM((16,) + cots[0].shape[1:], bf),
             pltpu.VMEM((2, count, HW, HALF), bf),
             pltpu.VMEM((8, HW, HALF), bf),
             pltpu.VMEM((8, SEQ, HALF), bf),
-            pltpu.SemaphoreType.DMA((20,)),
+            pltpu.VMEM((2, HW, HALF), bf),
+            pltpu.SemaphoreType.DMA((22,)),
         ],
         name="pair_scores",
         compiler_params=pltpu.CompilerParams(vmem_limit_bytes=56 * 2**20),
         cost_estimate=pl.CostEstimate(
             flops=2 * 16 * HW * HALF * SEQ * 4, bytes_accessed=20 * 2**20, transcendentals=0
         ),
-    )(*acts, *cots, *own_grads, *other_grads, own_fisher, other_fisher, ids.reshape(1, count), query_ids, layers)
+    )(*acts, *cots, *grads, own_fisher, other_fisher, ids.reshape(1, count), query_ids, layers)
 
 
 def offset_of(y, x):
@@ -221,7 +252,7 @@
     a = (2 * y + x // 2 + 4 * core) % 8
     head = 2 * ((z - a) % 8) + x % 2
     unit = lax.dynamic_slice_in_dim(query_output_cotangents[0], head * HW, HW, 1)
-    unit = jnp.pad(unit, ((0, -SEQ % 8), (0, 0)))
+    unit = pack(unit)
     unit = send(unit, lambda y, x, z, c: (y, x, z - offset_of(y, x) - 4 * c, c))
     other_fisher = send(fisher_diagonal_weight, swap)
     own_a = train_grad(train_cotangents, train_inputs, 0, CUTS[0])
@@ -230,12 +261,12 @@
     parts = [unit, send(unit, turn(1, True)), send(unit, turn(-1, True)), send(unit, turn(2, True))]
     other_a = send(own_a, swap)
     own_b = train_grad(train_cotangents, train_inputs, CUTS[0], CUTS[1])
+    other_b = send(own_b, swap)
     la, lb = stack(*parts[:2]), stack(*parts[2:])
     m3 = send(m2, up)
     p3 = send(p2, down)
     lpa, lpb = send(la, turn(1, False)), send(lb, turn(1, False))
     lma, lmb = send(la, turn(-1, False)), send(lb, turn(-1, False))
-    other_b = send(own_b, swap)
     far = lax.select(core == 0, m3, p3)
     f4 = send(far, lambda y, x, z, c: (y, x, z + 1 - 2 * c, c))
     l2a = send(lpa, turn(1, False))
@@ -243,18 +274,14 @@
     buckets = pair_scores(
         (own_x, p1, p2, p3, f4, m3, m2, m1),
         (la, lb, lpa, lpb, lma, lmb, l2a, l2b),
-        (own_a, own_b),
-        (other_a, other_b),
+        (own_a, own_b, other_a, other_b),
         fisher_diagonal_weight,
         other_fisher,
         train_ids,
         query_ids,
         layer_index,
     )
-    buckets = buckets[0] + send(buckets[1], swap)
-    shares = lax.all_to_all(
-        buckets.reshape(NY * NXL * NXH, 4, QIDS), ("y", "xlo", "xhi"), 0, 0, tiled=True
-    )
+    shares = lax.all_to_all(buckets, ("y", "xlo", "xhi", "core"), 0, 0, tiled=True)
     return jnp.sum(shares, axis=0)[:, :, None]
 
 

time: 108 us -> 106 us (0.981)
  blocking collectives: 9.18 us -> 19.1 us
  starting transfers between devices: 46.7 us -> 37.6 us
    all_to_all x1, blocking collectives: 9.18 us -> 19.1 us  [local(): lax.all_to_all(buckets, ('y', 'xlo', 'xhi', 'core'), 0, 0, tiled=True)]
    ppermute x21 -> x20, starting transfers between devices: 46.7 us -> 37.6 us  [send(): lax.ppermute(value, AXES, [(flat(*p), flat(*to(*p))) for p in places])]
    ppermute x21 -> x20, waiting for transfers between devices: 24.9 us -> 23.9 us  [send(): lax.ppermute(value, AXES, [(flat(*p), flat(*to(*p))) for p in places])]
    pallas_call x1 -> x2, Pallas kernels: 12.2 us -> 12 us  [the longest x1 11.9 us: pair_scores(): pl.pallas_call(functools.partial(pair_kernel, count), in_specs=[ANY] * 22...]
  transfers between devices with their start and end apart: 21 -> 20, of which waited for: 11 -> 10; matrix products, arithmetic and copies ran while one was open for 0% -> 0% of each run, Pallas kernels for 5% -> 5%
where the time goes in v1:
time: 106 us
  starting transfers between devices  37.6 us (35%)
  waiting for transfers between devices  23.9 us (23%)
  Pallas kernels  22.9 us (22%)
  blocking collectives  19.1 us (18%)
  local copies, waits for them, and re-layouts  1.59 us (2%)
    ppermute x20, starting transfers between devices, send(): lax.ppermute(value, AXES, [(flat(*p), flat(*to(*p))) for p in places])  37.6 us
    ppermute x20, waiting for transfers between devices, send(): lax.ppermute(value, AXES, [(flat(*p), flat(*to(*p))) for p in places])  23.9 us
    all_to_all x1, blocking collectives, local(): lax.all_to_all(buckets, ('y', 'xlo', 'xhi', 'core'), 0, 0, tiled=True)  19.1 us
    pallas_call x1, Pallas kernels, pair_scores(): pl.pallas_call(functools.partial(pair_kernel, count), in_specs=[ANY] * 22...  11.9 us
    pallas_call x2, Pallas kernels, train_grad(): pl.pallas_call(functools.partial(train_kernel, first, group), in_specs=[A...  10.9 us
  transfers between devices with their start and end apart: 20, of which 10 were waited for; matrix products, arithmetic and copies ran while one was open for 0% of the time, Pallas kernels for 5%

profile of v1, /device:TPU:1, one launch (start us, length us, event | category | flops | bytes accessed | tf_op | source)
XLA Modules:
  0.0 106.0 jit_solution(14023527216431814618)
XLA Ops:
  0.0 0.0 copy-start
  0.0 5.5 %train_grad.2.refs_16_ = bf16[11,240,640]{2,1,0:T(8,128)(2,1)} custom-call(bf16[22,257,240]{2,1,0:T(8,128)(2,1)} %cot_hbm.3, bf16[22,257,640]{2,1,0:T(8,128)(2,1)} %act_hbm.3), custom_call_target="tpu_custom_call" | custom-call | flops 3473817600 | bytes 8354720 | tf_op jit(solution)/shard_map/train_grad/pallas_call | solution.py:68
  5.5 0.0 copy-start.5
  5.5 3.3 %collective-permute-start.17 = (bf16[11,240,640]{2,1,0:T(8,128)(2,1)}, bf16[11,240,640]{2,1,0:T(8,128)(2,1)}, u32[]{:S(2)}, u32[]{:S(2)}) collective-permute-start(bf16[11,240,640]{2,1,0:T(8,128)(2,1)} %train_grad.2.refs_16_), channel_id=1, source_target_pairs={{0,2},{2,0},{4,6},{6,4},{8,10},{10,8},{12,14},{14,12},{16,18},{18,... | collective-permute-start | bytes 10137608 | tf_op jit(solution)/shard_map/ppermute | solution.py:35
  8.8 5.4 %train_grad.3.refs_17_ = bf16[11,240,640]{2,1,0:T(8,128)(2,1)} custom-call(bf16[22,257,240]{2,1,0:T(8,128)(2,1)} %cot_hbm.3, bf16[22,257,640]{2,1,0:T(8,128)(2,1)} %act_hbm.3), custom_call_target="tpu_custom_call" | custom-call | flops 3473817600 | bytes 8354720 | tf_op jit(solution)/shard_map/train_grad/pallas_call | solution.py:68
  14.2 0.1 collective-permute-start.18
  14.3 0.0 copy-done
  14.4 0.1 dynamic-slice_bitcast_fusion.cot_ref
  14.5 0.1 pack.1
  14.6 7.1 %collective-permute-start.7 = (bf16[248,256]{1,0:T(8,128)(2,1)S(1)}, bf16[248,256]{1,0:T(8,128)(2,1)S(1)}, u32[]{:S(2)}, u32[]{:S(2)}) collective-permute-start(bf16[248,256]{1,0:T(8,128)(2,1)S(1)} %pack.1), channel_id=1, source_target_pairs={{0,0},{2,18},{4,4},{6,22},{8,8},{10,26},{12,12},{14,30},{16,16},{1... | collective-permute-start | bytes 380936 | tf_op jit(solution)/shard_map/ppermute | solution.py:35
  21.7 2.6 %collective-permute-done.7.refs_0_ = bf16[248,256]{1,0:T(8,128)(2,1)S(1)} collective-permute-done((bf16[248,256]{1,0:T(8,128)(2,1)S(1)}, bf16[248,256]{1,0:T(8,128)(2,1)S(1)}, u32[]{:S(2)}, u32[]{:S(2)}) %collective-permute-start.7) | collective-permute-done | bytes 127008 | tf_op jit(solution)/shard_map/ppermute | solution.py:35
  24.2 0.0 collective-permute-start.10
  24.2 2.6 %collective-permute-start.8 = (bf16[248,256]{1,0:T(8,128)(2,1)S(1)}, bf16[248,256]{1,0:T(8,128)(2,1)S(1)}, u32[]{:S(2)}, u32[]{:S(2)}) collective-permute-start(bf16[248,256]{1,0:T(8,128)(2,1)S(1)} %collective-permute-done.7.refs_0_), channel_id=1, source_target_pairs={{0,33},{2,194},{4,37},{6,198},{8,41},{10,202},{12,45},{14,206},{16... | collective-permute-start | bytes 380936 | tf_op jit(solution)/shard_map/ppermute | solution.py:35
  26.9 0.0 copy-done.5
  26.9 2.0 %collective-permute-start.3 = (bf16[257,640]{1,0:T(8,128)(2,1)S(1)}, bf16[257,640]{1,0:T(8,128)(2,1)S(1)}, u32[]{:S(2)}, u32[]{:S(2)}) collective-permute-start(bf16[257,640]{1,0:T(8,128)(2,1)S(1)} %bitcast.8), channel_id=1, source_target_pairs={{0,4},{2,6},{4,8},{6,10},{8,12},{10,14},{12,16},{14,18},{16,20},{1... | collective-permute-start | bytes 986888 | tf_op jit(solution)/shard_map/ppermute | solution.py:35
  28.9 0.6 collective-permute-done.10.refs_1_
  29.5 4.1 %collective-permute-start = (bf16[257,640]{1,0:T(8,128)(2,1)S(1)}, bf16[257,640]{1,0:T(8,128)(2,1)S(1)}, u32[]{:S(2)}, u32[]{:S(2)}) collective-permute-start(bf16[257,640]{1,0:T(8,128)(2,1)S(1)} %bitcast.9), channel_id=1, source_target_pairs={{0,28},{2,30},{4,0},{6,2},{8,4},{10,6},{12,8},{14,10},{16,12},{18,... | collective-permute-start | bytes 986888 | tf_op jit(solution)/shard_map/ppermute | solution.py:35
  33.6 0.0 collective-permute-done.8.refs_1_
  33.6 0.0 collective-permute-start.9
  33.6 0.0 copy-start.1
  33.6 5.2 %collective-permute-done.9.refs_0_ = bf16[248,256]{1,0:T(8,128)(2,1)S(1)} collective-permute-done((bf16[248,256]{1,0:T(8,128)(2,1)S(1)}, bf16[248,256]{1,0:T(8,128)(2,1)S(1)}, u32[]{:S(2)}, u32[]{:S(2)}) %collective-permute-start.9) | collective-permute-done | bytes 127008 | tf_op jit(solution)/shard_map/ppermute | solution.py:35
  38.9 1.2 %collective-permute-start.13 = (bf16[2,248,256]{2,1,0:T(8,128)(2,1)S(1)}, bf16[2,248,256]{2,1,0:T(8,128)(2,1)S(1)}, u32[]{:S(2)}, u32[]{:S(2)}) collective-permute-start(bf16[2,248,256]{2,1,0:T(8,128)(2,1)S(1)} %stack.2.refs_8_), channel_id=1, source_target_pairs={{0,64},{2,34},{4,68},{6,38},{8,72},{10,42},{12,76},{14,46},{16,80}... | collective-permute-start | bytes 761864 | tf_op jit(solution)/shard_map/ppermute | solution.py:35
  40.0 0.0 collective-permute-done.3.refs_7_
  40.1 0.0 collective-permute-start.4
  40.1 1.0 collective-permute-done.refs_1_
  41.0 3.1 %collective-permute-start.1 = (bf16[257,640]{1,0:T(8,128)(2,1)S(1)}, bf16[257,640]{1,0:T(8,128)(2,1)S(1)}, u32[]{:S(2)}, u32[]{:S(2)}) collective-permute-start(bf16[257,640]{1,0:T(8,128)(2,1)S(1)} %collective-permute-done.refs_1_), channel_id=1, source_target_pairs={{0,28},{2,30},{4,0},{6,2},{8,4},{10,6},{12,8},{14,10},{16,12},{18,... | collective-permute-start | bytes 986888 | tf_op jit(solution)/shard_map/ppermute | solution.py:35
  44.1 1.4 %collective-permute-done.13.refs_12_ = bf16[2,248,256]{2,1,0:T(8,128)(2,1)S(1)} collective-permute-done((bf16[2,248,256]{2,1,0:T(8,128)(2,1)S(1)}, bf16[2,248,256]{2,1,0:T(8,128)(2,1)S(1)}, u32[]{:S(2)}, u32[]{:S(2)}) %collective-permute-start.13) | collective-permute-done | bytes 253984 | tf_op jit(solution)/shard_map/ppermute | solution.py:35
  45.5 0.5 collective-permute-start.11
  46.0 0.0 copy-done.6
  46.0 1.6 %collective-permute-done.4.refs_6_ = bf16[257,640]{1,0:T(8,128)(2,1)S(1)} collective-permute-done((bf16[257,640]{1,0:T(8,128)(2,1)S(1)}, bf16[257,640]{1,0:T(8,128)(2,1)S(1)}, u32[]{:S(2)}, u32[]{:S(2)}) %collective-permute-start.4) | collective-permute-done | bytes 328992 | tf_op jit(solution)/shard_map/ppermute | solution.py:35
  47.6 0.0 collective-permute-start.5
  47.6 0.0 copy-done.7
  47.6 1.3 %collective-permute-done.1.refs_2_ = bf16[257,640]{1,0:T(8,128)(2,1)S(1)} collective-permute-done((bf16[257,640]{1,0:T(8,128)(2,1)S(1)}, bf16[257,640]{1,0:T(8,128)(2,1)S(1)}, u32[]{:S(2)}, u32[]{:S(2)}) %collective-permute-start.1) | collective-permute-done | bytes 328992 | tf_op jit(solution)/shard_map/ppermute | solution.py:35
  49.0 3.4 %collective-permute-start.2 = (bf16[257,640]{1,0:T(8,128)(2,1)S(1)}, bf16[257,640]{1,0:T(8,128)(2,1)S(1)}, u32[]{:S(2)}, u32[]{:S(2)}) collective-permute-start(bf16[257,640]{1,0:T(8,128)(2,1)S(1)} %collective-permute-done.1.refs_2_), channel_id=1, source_target_pairs={{0,28},{2,30},{4,0},{6,2},{8,4},{10,6},{12,8},{14,10},{16,12},{18,... | collective-permute-start | bytes 986888 | tf_op jit(solution)/shard_map/ppermute | solution.py:35
  52.4 0.0 collective-permute-done.11.refs_10_
  52.4 0.0 copy-done.11
  52.4 0.7 copy-done.12
  53.1 3.6 %collective-permute-start.19 = (bf16[2,240,640]{2,1,0:T(8,128)(2,1)}, bf16[2,240,640]{2,1,0:T(8,128)(2,1)}, u32[]{:S(2)}, u32[]{:S(2)}) collective-permute-start(bf16[2,240,640]{2,1,0:T(8,128)(2,1)} %refs_20_.1), channel_id=1, source_target_pairs={{0,2},{2,0},{4,6},{6,4},{8,10},{10,8},{12,14},{14,12},{16,18},{18,... | collective-permute-start | bytes 1843208 | tf_op jit(solution)/shard_map/ppermute | solution.py:35
  56.7 0.0 copy-start.2
  56.7 0.0 collective-permute-done.5.refs_5_
  56.7 0.0 copy-done.8
  56.7 0.0 copy-start.3
  56.7 0.7 collective-permute-start.14
  57.4 0.0 collective-permute-done.2.refs_3_
  57.4 2.7 %collective-permute-start.12 = (bf16[2,248,256]{2,1,0:T(8,128)(2,1)S(1)}, bf16[2,248,256]{2,1,0:T(8,128)(2,1)S(1)}, u32[]{:S(2)}, u32[]{:S(2)}) collective-permute-start(bf16[2,248,256]{2,1,0:T(8,128)(2,1)S(1)} %stack.3.refs_9_), channel_id=1, source_target_pairs={{0,192},{2,35},{4,196},{6,39},{8,200},{10,43},{12,204},{14,47},{16... | collective-permute-start | bytes 761864 | tf_op jit(solution)/shard_map/ppermute | solution.py:35
  60.2 3.6 %collective-permute-done.14.refs_13_ = bf16[2,248,256]{2,1,0:T(8,128)(2,1)} collective-permute-done((bf16[2,248,256]{2,1,0:T(8,128)(2,1)S(1)}, bf16[2,248,256]{2,1,0:T(8,128)(2,1)}, u32[]{:S(2)}, u32[]{:S(2)}) %collective-permute-start.14) | collective-permute-done | bytes 253984 | tf_op jit(solution)/shard_map/ppermute | solution.py:35
  63.9 1.5 %collective-permute-start.6 = (bf16[257,640]{1,0:T(8,128)(2,1)S(1)}, bf16[257,640]{1,0:T(8,128)(2,1)S(1)}, u32[]{:S(2)}, u32[]{:S(2)}) collective-permute-start(bf16[257,640]{1,0:T(8,128)(2,1)S(1)} %broadcast_select_fusion), channel_id=1, source_target_pairs={{0,4},{2,30},{4,8},{6,2},{8,12},{10,6},{12,16},{14,10},{16,20},{18... | collective-permute-start | bytes 986888 | tf_op jit(solution)/shard_map/ppermute | solution.py:35
  65.4 0.0 collective-permute-done.12.refs_11_
  65.4 1.6 %collective-permute-start.15 = (bf16[2,248,256]{2,1,0:T(8,128)(2,1)}, bf16[2,248,256]{2,1,0:T(8,128)(2,1)S(1)}, u32[]{:S(2)}, u32[]{:S(2)}) collective-permute-start(bf16[2,248,256]{2,1,0:T(8,128)(2,1)} %copy-done.12), channel_id=1, source_target_pairs={{0,192},{2,35},{4,196},{6,39},{8,200},{10,43},{12,204},{14,47},{16... | collective-permute-start | bytes 761864 | tf_op jit(solution)/shard_map/ppermute | solution.py:35
  67.0 0.0 collective-permute-done.19.refs_21_
  67.0 0.0 collective-permute-start.16
  67.0 4.0 %collective-permute-done.15.refs_14_ = bf16[2,248,256]{2,1,0:T(8,128)(2,1)S(1)} collective-permute-done((bf16[2,248,256]{2,1,0:T(8,128)(2,1)}, bf16[2,248,256]{2,1,0:T(8,128)(2,1)S(1)}, u32[]{:S(2)}, u32[]{:S(2)}) %collective-permute-start.15) | collective-permute-done | bytes 253984 | tf_op jit(solution)/shard_map/ppermute | solution.py:35
  71.0 2.5 %collective-permute-done.16.refs_15_ = bf16[2,248,256]{2,1,0:T(8,128)(2,1)S(1)} collective-permute-done((bf16[2,248,256]{2,1,0:T(8,128)(2,1)}, bf16[2,248,256]{2,1,0:T(8,128)(2,1)S(1)}, u32[]{:S(2)}, u32[]{:S(2)}) %collective-permute-start.16) | collective-permute-done | bytes 253984 | tf_op jit(solution)/shard_map/ppermute | solution.py:35
  73.5 0.0 collective-permute-done.6.refs_4_
  73.5 0.0 collective-permute-done.17.refs_18_
  73.5 0.0 collective-permute-done.18.refs_19_
  73.5 0.0 copy-done.1
  73.5 0.0 copy-done.9
  73.6 0.0 copy-done.2
  73.6 0.6 copy-done.15
  74.2 0.1 copy-done.10
  74.3 11.9 %pair_scores.1 = f32[32,4,16]{2,1,0:T(4,128)} custom-call(bf16[257,640]{1,0:T(8,128)(2,1)} %bitcast.7, bf16[257,640]{1,0:T(8,128)(2,1)} %copy-done.7, bf16[257,640]{1,0:T(8,128)(2,1)} %copy-done.9, bf16[257,640]{1,0:T(8,128)(2,1)} %copy-done.4, bf16[257,640]{1,0:T(8,128)(2,1)} %copy-done.10, bf16[257,640]{1,0:T(8,128)(2,1)} %copy-done.3, ...), custom_call_target="tpu_custom_call" | custom-call | flops 5052825600 | bytes 20971520 | tf_op jit(solution)/shard_map/pair_scores/pallas_call | solution.py:202
  86.3 19.1 %all_to_all.5 = f32[32,4,16]{2,1,0:T(4,128)S(1)} all-to-all(f32[32,4,16]{2,1,0:T(4,128)} %pair_scores.1), channel_id=1, replica_groups=mesh['y'=4,'xlo'=2,'z'=8,'core'=2,'xhi'=2] {'y','xlo','xhi','core'}, dimensions={0} | all-to-all | bytes 16384 | tf_op jit(solution)/shard_map/all_to_all | solution.py:284
  105.3 0.6 reduce_sum.9
  (18 shorter events, 0.1 us)
Async XLA Ops:
  0.0 14.3 %copy-start = (bf16[1,257,3840]{2,1,0:T(8,128)(2,1)S(1)}, bf16[1,257,3840]{2,1,0:T(8,128)(2,1)}, u32[]{:S(2)}) copy-start(bf16[1,257,3840]{2,1,0:T(8,128)(2,1)} %param.12) | copy-start | bytes 5921284
  5.5 21.4 %copy-start.5 = (bf16[1,257,640]{2,1,0:T(8,128)(2,1)S(1)}, bf16[1,257,640]{2,1,0:T(8,128)(2,1)}, u32[]{:S(2)}) copy-start(bf16[1,257,640]{2,1,0:T(8,128)(2,1)} %param.11) | copy-start | bytes 986884
  5.5 68.0 %collective-permute-start.17 = (bf16[11,240,640]{2,1,0:T(8,128)(2,1)}, bf16[11,240,640]{2,1,0:T(8,128)(2,1)}, u32[]{:S(2)}, u32[]{:S(2)}) collective-permute-start(bf16[11,240,640]{2,1,0:T(8,128)(2,1)} %train_grad.2.refs_16_), channel_id=1, source_target_pairs={{0,2},{2,0},{4,6},{6,4},{8,10},{10,8},{12,14},{14,12},{16,18},{18,... | collective-permute-start | bytes 10137608 | tf_op jit(solution)/shard_map/ppermute | solution.py:35
  14.2 59.4 %collective-permute-start.18 = (bf16[11,240,640]{2,1,0:T(8,128)(2,1)}, bf16[11,240,640]{2,1,0:T(8,128)(2,1)}, u32[]{:S(2)}, u32[]{:S(2)}) collective-permute-start(bf16[11,240,640]{2,1,0:T(8,128)(2,1)} %train_grad.3.refs_17_), channel_id=1, source_target_pairs={{0,2},{2,0},{4,6},{6,4},{8,10},{10,8},{12,14},{14,12},{16,18},{18,... | collective-permute-start | bytes 10137608 | tf_op jit(solution)/shard_map/ppermute | solution.py:35
  14.6 9.7 %collective-permute-start.7 = (bf16[248,256]{1,0:T(8,128)(2,1)S(1)}, bf16[248,256]{1,0:T(8,128)(2,1)S(1)}, u32[]{:S(2)}, u32[]{:S(2)}) collective-permute-start(bf16[248,256]{1,0:T(8,128)(2,1)S(1)} %pack.1), channel_id=1, source_target_pairs={{0,0},{2,18},{4,4},{6,22},{8,8},{10,26},{12,12},{14,30},{16,16},{1... | collective-permute-start | bytes 380936 | tf_op jit(solution)/shard_map/ppermute | solution.py:35
  24.2 5.3 %collective-permute-start.10 = (bf16[248,256]{1,0:T(8,128)(2,1)S(1)}, bf16[248,256]{1,0:T(8,128)(2,1)S(1)}, u32[]{:S(2)}, u32[]{:S(2)}) collective-permute-start(bf16[248,256]{1,0:T(8,128)(2,1)S(1)} %collective-permute-done.7.refs_0_), channel_id=1, source_target_pairs={{0,1},{2,130},{4,5},{6,134},{8,9},{10,138},{12,13},{14,142},{16,17... | collective-permute-start | bytes 380936 | tf_op jit(solution)/shard_map/ppermute | solution.py:35
  24.2 9.3 %collective-permute-start.8 = (bf16[248,256]{1,0:T(8,128)(2,1)S(1)}, bf16[248,256]{1,0:T(8,128)(2,1)S(1)}, u32[]{:S(2)}, u32[]{:S(2)}) collective-permute-start(bf16[248,256]{1,0:T(8,128)(2,1)S(1)} %collective-permute-done.7.refs_0_), channel_id=1, source_target_pairs={{0,33},{2,194},{4,37},{6,198},{8,41},{10,202},{12,45},{14,206},{16... | collective-permute-start | bytes 380936 | tf_op jit(solution)/shard_map/ppermute | solution.py:35
  26.9 13.2 %collective-permute-start.3 = (bf16[257,640]{1,0:T(8,128)(2,1)S(1)}, bf16[257,640]{1,0:T(8,128)(2,1)S(1)}, u32[]{:S(2)}, u32[]{:S(2)}) collective-permute-start(bf16[257,640]{1,0:T(8,128)(2,1)S(1)} %bitcast.8), channel_id=1, source_target_pairs={{0,4},{2,6},{4,8},{6,10},{8,12},{10,14},{12,16},{14,18},{16,20},{1... | collective-permute-start | bytes 986888 | tf_op jit(solution)/shard_map/ppermute | solution.py:35
  29.5 11.5 %collective-permute-start = (bf16[257,640]{1,0:T(8,128)(2,1)S(1)}, bf16[257,640]{1,0:T(8,128)(2,1)S(1)}, u32[]{:S(2)}, u32[]{:S(2)}) collective-permute-start(bf16[257,640]{1,0:T(8,128)(2,1)S(1)} %bitcast.9), channel_id=1, source_target_pairs={{0,28},{2,30},{4,0},{6,2},{8,4},{10,6},{12,8},{14,10},{16,12},{18,... | collective-permute-start | bytes 986888 | tf_op jit(solution)/shard_map/ppermute | solution.py:35
  33.6 5.3 %collective-permute-start.9 = (bf16[248,256]{1,0:T(8,128)(2,1)S(1)}, bf16[248,256]{1,0:T(8,128)(2,1)S(1)}, u32[]{:S(2)}, u32[]{:S(2)}) collective-permute-start(bf16[248,256]{1,0:T(8,128)(2,1)S(1)} %collective-permute-done.7.refs_0_), channel_id=1, source_target_pairs={{0,32},{2,66},{4,36},{6,70},{8,40},{10,74},{12,44},{14,78},{16,48}... | collective-permute-start | bytes 380936 | tf_op jit(solution)/shard_map/ppermute | solution.py:35
  33.6 39.9 %copy-start.1 = (bf16[2,248,256]{2,1,0:T(8,128)(2,1)}, bf16[2,248,256]{2,1,0:T(8,128)(2,1)S(1)}, u32[]{:S(2)}) copy-start(bf16[2,248,256]{2,1,0:T(8,128)(2,1)S(1)} %stack.2.refs_8_) | copy-start | bytes 761860
  38.9 6.6 %collective-permute-start.13 = (bf16[2,248,256]{2,1,0:T(8,128)(2,1)S(1)}, bf16[2,248,256]{2,1,0:T(8,128)(2,1)S(1)}, u32[]{:S(2)}, u32[]{:S(2)}) collective-permute-start(bf16[2,248,256]{2,1,0:T(8,128)(2,1)S(1)} %stack.2.refs_8_), channel_id=1, source_target_pairs={{0,64},{2,34},{4,68},{6,38},{8,72},{10,42},{12,76},{14,46},{16,80}... | collective-permute-start | bytes 761864 | tf_op jit(solution)/shard_map/ppermute | solution.py:35
  40.1 5.9 %copy-start.6 = (bf16[257,640]{1,0:T(8,128)(2,1)}, bf16[257,640]{1,0:T(8,128)(2,1)S(1)}, u32[]{:S(2)}) copy-start(bf16[257,640]{1,0:T(8,128)(2,1)S(1)} %collective-permute-done.3.refs_7_) | copy-start | bytes 986884
  40.1 7.5 %collective-permute-start.4 = (bf16[257,640]{1,0:T(8,128)(2,1)S(1)}, bf16[257,640]{1,0:T(8,128)(2,1)S(1)}, u32[]{:S(2)}, u32[]{:S(2)}) collective-permute-start(bf16[257,640]{1,0:T(8,128)(2,1)S(1)} %collective-permute-done.3.refs_7_), channel_id=1, source_target_pairs={{0,4},{2,6},{4,8},{6,10},{8,12},{10,14},{12,16},{14,18},{16,20},{1... | collective-permute-start | bytes 986888 | tf_op jit(solution)/shard_map/ppermute | solution.py:35
  41.0 6.6 %copy-start.7 = (bf16[257,640]{1,0:T(8,128)(2,1)}, bf16[257,640]{1,0:T(8,128)(2,1)S(1)}, u32[]{:S(2)}) copy-start(bf16[257,640]{1,0:T(8,128)(2,1)S(1)} %collective-permute-done.refs_1_) | copy-start | bytes 986884
  41.0 7.9 %collective-permute-start.1 = (bf16[257,640]{1,0:T(8,128)(2,1)S(1)}, bf16[257,640]{1,0:T(8,128)(2,1)S(1)}, u32[]{:S(2)}, u32[]{:S(2)}) collective-permute-start(bf16[257,640]{1,0:T(8,128)(2,1)S(1)} %collective-permute-done.refs_1_), channel_id=1, source_target_pairs={{0,28},{2,30},{4,0},{6,2},{8,4},{10,6},{12,8},{14,10},{16,12},{18,... | collective-permute-start | bytes 986888 | tf_op jit(solution)/shard_map/ppermute | solution.py:35
  45.5 6.9 %copy-start.11 = (bf16[2,248,256]{2,1,0:T(8,128)(2,1)}, bf16[2,248,256]{2,1,0:T(8,128)(2,1)S(1)}, u32[]{:S(2)}) copy-start(bf16[2,248,256]{2,1,0:T(8,128)(2,1)S(1)} %collective-permute-done.13.refs_12_) | copy-start | bytes 761860
  45.5 6.9 %collective-permute-start.11 = (bf16[2,248,256]{2,1,0:T(8,128)(2,1)S(1)}, bf16[2,248,256]{2,1,0:T(8,128)(2,1)S(1)}, u32[]{:S(2)}, u32[]{:S(2)}) collective-permute-start(bf16[2,248,256]{2,1,0:T(8,128)(2,1)S(1)} %stack.2.refs_8_), channel_id=1, source_target_pairs={{0,192},{2,35},{4,196},{6,39},{8,200},{10,43},{12,204},{14,47},{16... | collective-permute-start | bytes 761864 | tf_op jit(solution)/shard_map/ppermute | solution.py:35
  47.6 9.1 %copy-start.8 = (bf16[257,640]{1,0:T(8,128)(2,1)}, bf16[257,640]{1,0:T(8,128)(2,1)S(1)}, u32[]{:S(2)}) copy-start(bf16[257,640]{1,0:T(8,128)(2,1)S(1)} %collective-permute-done.4.refs_6_) | copy-start | bytes 986884
  47.6 9.1 %collective-permute-start.5 = (bf16[257,640]{1,0:T(8,128)(2,1)S(1)}, bf16[257,640]{1,0:T(8,128)(2,1)S(1)}, u32[]{:S(2)}, u32[]{:S(2)}) collective-permute-start(bf16[257,640]{1,0:T(8,128)(2,1)S(1)} %collective-permute-done.4.refs_6_), channel_id=1, source_target_pairs={{0,4},{2,6},{4,8},{6,10},{8,12},{10,14},{12,16},{14,18},{16,20},{1... | collective-permute-start | bytes 986888 | tf_op jit(solution)/shard_map/ppermute | solution.py:35
  49.0 24.6 %copy-start.9 = (bf16[257,640]{1,0:T(8,128)(2,1)}, bf16[257,640]{1,0:T(8,128)(2,1)S(1)}, u32[]{:S(2)}) copy-start(bf16[257,640]{1,0:T(8,128)(2,1)S(1)} %collective-permute-done.1.refs_2_) | copy-start | bytes 986884
  49.0 8.5 %collective-permute-start.2 = (bf16[257,640]{1,0:T(8,128)(2,1)S(1)}, bf16[257,640]{1,0:T(8,128)(2,1)S(1)}, u32[]{:S(2)}, u32[]{:S(2)}) collective-permute-start(bf16[257,640]{1,0:T(8,128)(2,1)S(1)} %collective-permute-done.1.refs_2_), channel_id=1, source_target_pairs={{0,28},{2,30},{4,0},{6,2},{8,4},{10,6},{12,8},{14,10},{16,12},{18,... | collective-permute-start | bytes 986888 | tf_op jit(solution)/shard_map/ppermute | solution.py:35
  52.4 0.7 copy-start.12
  53.1 13.9 %collective-permute-start.19 = (bf16[2,240,640]{2,1,0:T(8,128)(2,1)}, bf16[2,240,640]{2,1,0:T(8,128)(2,1)}, u32[]{:S(2)}, u32[]{:S(2)}) collective-permute-start(bf16[2,240,640]{2,1,0:T(8,128)(2,1)} %refs_20_.1), channel_id=1, source_target_pairs={{0,2},{2,0},{4,6},{6,4},{8,10},{10,8},{12,14},{14,12},{16,18},{18,... | collective-permute-start | bytes 1843208 | tf_op jit(solution)/shard_map/ppermute | solution.py:35
  56.7 16.9 %copy-start.2 = (bf16[2,248,256]{2,1,0:T(8,128)(2,1)}, bf16[2,248,256]{2,1,0:T(8,128)(2,1)S(1)}, u32[]{:S(2)}) copy-start(bf16[2,248,256]{2,1,0:T(8,128)(2,1)S(1)} %stack.3.refs_9_) | copy-start | bytes 761860
  56.7 16.8 %copy-start.3 = (bf16[257,640]{1,0:T(8,128)(2,1)}, bf16[257,640]{1,0:T(8,128)(2,1)S(1)}, u32[]{:S(2)}) copy-start(bf16[257,640]{1,0:T(8,128)(2,1)S(1)} %collective-permute-done.5.refs_5_) | copy-start | bytes 986884
  56.7 7.1 %collective-permute-start.14 = (bf16[2,248,256]{2,1,0:T(8,128)(2,1)S(1)}, bf16[2,248,256]{2,1,0:T(8,128)(2,1)}, u32[]{:S(2)}, u32[]{:S(2)}) collective-permute-start(bf16[2,248,256]{2,1,0:T(8,128)(2,1)S(1)} %stack.3.refs_9_), channel_id=1, source_target_pairs={{0,64},{2,34},{4,68},{6,38},{8,72},{10,42},{12,76},{14,46},{16,80}... | collective-permute-start | bytes 761864 | tf_op jit(solution)/shard_map/ppermute | solution.py:35
  57.4 16.1 %copy-start.4 = (bf16[257,640]{1,0:T(8,128)(2,1)}, bf16[257,640]{1,0:T(8,128)(2,1)S(1)}, u32[]{:S(2)}) copy-start(bf16[257,640]{1,0:T(8,128)(2,1)S(1)} %collective-permute-done.2.refs_3_) | copy-start | bytes 986884
  57.4 7.9 %collective-permute-start.12 = (bf16[2,248,256]{2,1,0:T(8,128)(2,1)S(1)}, bf16[2,248,256]{2,1,0:T(8,128)(2,1)S(1)}, u32[]{:S(2)}, u32[]{:S(2)}) collective-permute-start(bf16[2,248,256]{2,1,0:T(8,128)(2,1)S(1)} %stack.3.refs_9_), channel_id=1, source_target_pairs={{0,192},{2,35},{4,196},{6,39},{8,200},{10,43},{12,204},{14,47},{16... | collective-permute-start | bytes 761864 | tf_op jit(solution)/shard_map/ppermute | solution.py:35
  63.9 9.7 %collective-permute-start.6 = (bf16[257,640]{1,0:T(8,128)(2,1)S(1)}, bf16[257,640]{1,0:T(8,128)(2,1)S(1)}, u32[]{:S(2)}, u32[]{:S(2)}) collective-permute-start(bf16[257,640]{1,0:T(8,128)(2,1)S(1)} %broadcast_select_fusion), channel_id=1, source_target_pairs={{0,4},{2,30},{4,8},{6,2},{8,12},{10,6},{12,16},{14,10},{16,20},{18... | collective-permute-start | bytes 986888 | tf_op jit(solution)/shard_map/ppermute | solution.py:35
  65.4 8.2 %copy-start.13 = (bf16[2,248,256]{2,1,0:T(8,128)(2,1)}, bf16[2,248,256]{2,1,0:T(8,128)(2,1)S(1)}, u32[]{:S(2)}) copy-start(bf16[2,248,256]{2,1,0:T(8,128)(2,1)S(1)} %collective-permute-done.12.refs_11_) | copy-start | bytes 761860
  65.4 5.6 %collective-permute-start.15 = (bf16[2,248,256]{2,1,0:T(8,128)(2,1)}, bf16[2,248,256]{2,1,0:T(8,128)(2,1)S(1)}, u32[]{:S(2)}, u32[]{:S(2)}) collective-permute-start(bf16[2,248,256]{2,1,0:T(8,128)(2,1)} %copy-done.12), channel_id=1, source_target_pairs={{0,192},{2,35},{4,196},{6,39},{8,200},{10,43},{12,204},{14,47},{16... | collective-permute-start | bytes 761864 | tf_op jit(solution)/shard_map/ppermute | solution.py:35
  67.0 6.6 %collective-permute-start.16 = (bf16[2,248,256]{2,1,0:T(8,128)(2,1)}, bf16[2,248,256]{2,1,0:T(8,128)(2,1)S(1)}, u32[]{:S(2)}, u32[]{:S(2)}) collective-permute-start(bf16[2,248,256]{2,1,0:T(8,128)(2,1)} %collective-permute-done.14.refs_13_), channel_id=1, source_target_pairs={{0,64},{2,34},{4,68},{6,38},{8,72},{10,42},{12,76},{14,46},{16,80}... | collective-permute-start | bytes 761864 | tf_op jit(solution)/shard_map/ppermute | solution.py:35
  71.0 2.6 %copy-start.14 = (bf16[2,248,256]{2,1,0:T(8,128)(2,1)}, bf16[2,248,256]{2,1,0:T(8,128)(2,1)S(1)}, u32[]{:S(2)}) copy-start(bf16[2,248,256]{2,1,0:T(8,128)(2,1)S(1)} %collective-permute-done.15.refs_14_) | copy-start | bytes 761860
  73.5 0.7 copy-start.15
  73.5 0.8 copy-start.10

commit v2 on v1

--- a/solution.py
+++ b/solution.py
@@ -10,6 +10,7 @@
 
 D = 1280
 HEAD_DIM = 80
+HEADS = 16
 SEQ = 257
 BODY = 256
 TIDS = 64
@@ -17,13 +18,12 @@
 HW = 3 * HEAD_DIM
 HALF = D // 2
 ROWS = 16
-CUTS = (11, 11)
+CUTS = (10, 12)
 NY, NXL, NZ, NC, NXH = 4, 2, 8, 2, 2
 AXES = ("y", "xlo", "z", "core", "xhi")
 SCALE = 1.0 / (SEQ * math.sqrt(HW * D))
 ANY = pl.BlockSpec(memory_space=pl.ANY)
 VMEM = pl.BlockSpec(memory_space=pltpu.VMEM)
-SMEM = pl.BlockSpec(memory_space=pltpu.SMEM)
 
 
 def flat(y, x, z, c):
@@ -43,24 +43,29 @@
     return body + column * act[BODY:SEQ].astype(jnp.float32)
 
 
-def train_kernel(first, group, cot_hbm, act_hbm, out_ref, cot, act, sems):
-    count = out_ref.shape[0]
+def train_kernel(first, group, cot_hbm, act_hbm, out_hbm, cot, act, out, sems):
+    count = out.shape[0]
     copies = []
     for i in range(0, count, group):
-        size = min(group, count - i)
-        src, dst = pl.ds(first + i, size), pl.ds(i, size)
-        pair = (
-            pltpu.make_async_copy(cot_hbm.at[src], cot.at[dst], sems.at[0, i // group]),
-            pltpu.make_async_copy(act_hbm.at[src], act.at[dst], sems.at[1, i // group]),
+        src, dst = pl.ds(first + i, group), pl.ds(i, group)
+        copies.append(
+            (
+                pltpu.make_async_copy(cot_hbm.at[src], cot.at[dst], sems.at[0, i // group]),
+                pltpu.make_async_copy(act_hbm.at[src], act.at[dst], sems.at[1, i // group]),
+                pltpu.make_async_copy(out.at[dst], out_hbm.at[dst], sems.at[2, i // group]),
+            )
         )
-        copies.append((i, size, pair))
-        for c in pair:
-            c.start()
-    for i, size, pair in copies:
-        for c in pair:
-            c.wait()
-        for j in range(i, i + size):
-            out_ref[j] = outer_sum(cot[j], act[j]).astype(jnp.bfloat16)
+    for c in copies:
+        c[0].start()
+        c[1].start()
+    for i, c in enumerate(copies):
+        c[0].wait()
+        c[1].wait()
+        for j in range(i * group, (i + 1) * group):
+            out[j] = outer_sum(cot[j], act[j]).astype(jnp.bfloat16)
+        c[2].start()
+    for c in copies:
+        c[2].wait()
 
 
 def train_grad(cot, act, first, count):
@@ -68,12 +73,13 @@
     return pl.pallas_call(
         functools.partial(train_kernel, first, group),
         in_specs=[ANY, ANY],
-        out_specs=VMEM,
+        out_specs=ANY,
         out_shape=jax.ShapeDtypeStruct((count, HW, HALF), jnp.bfloat16),
         scratch_shapes=[
             pltpu.VMEM((count, SEQ, HW), jnp.bfloat16),
             pltpu.VMEM((count, SEQ, HALF), jnp.bfloat16),
-            pltpu.SemaphoreType.DMA((2, -(-count // group))),
+            pltpu.VMEM((count, HW, HALF), jnp.bfloat16),
+            pltpu.SemaphoreType.DMA((3, count // group)),
         ],
         name="train_grad",
         compiler_params=pltpu.CompilerParams(vmem_limit_bytes=58 * 2**20),
@@ -129,33 +135,36 @@
 
 def pair_kernel(count_train, *refs):
     acts, refs = refs[:8], refs[8:]
-    cots, refs = refs[:8], refs[8:]
+    cots, refs = refs[:4], refs[4:]
     grads, refs = refs[:4], refs[4:]
-    own_fisher, other_fisher, ids_ref, query_ids, layer_index, out_ref = refs[:6]
-    cot, grad, weighted, act, chosen, sems = refs[6:]
+    own_fisher, other_fisher, table_ref, out_ref = refs[:4]
+    cot, grad, weighted, act, fishers, table, sems = refs[4:]
     core, z, y = lax.axis_index("core"), lax.axis_index("z"), lax.axis_index("y")
     x = lax.axis_index("xhi") * 2 + lax.axis_index("xlo")
     first = []
     for k, ref in enumerate(acts):
         first.append(pltpu.make_async_copy(ref, act.at[k], sems.at[k]))
     for i, ref in enumerate(cots):
-        first.append(pltpu.make_async_copy(ref, cot.at[pl.ds(2 * i, 2)], sems.at[8 + i]))
+        first.append(pltpu.make_async_copy(ref, cot.at[pl.ds(4 * i, 4)], sems.at[8 + i]))
     for e, ref in enumerate((own_fisher, other_fisher)):
-        layer = layer_index[2 * z + (core if e == 0 else 1 - core)]
-        first.append(pltpu.make_async_copy(ref.at[layer], chosen.at[e], sems.at[16 + e]))
+        first.append(pltpu.make_async_copy(ref, fishers.at[e], sems.at[16 + e]))
     later = []
     for i, ref in enumerate(grads):
         e, rows = i // 2, pl.ds((i % 2) * CUTS[0], ref.shape[0])
         later.append(pltpu.make_async_copy(ref, grad.at[e, rows], sems.at[18 + i]))
-    for c in first + later:
+    numbers = pltpu.make_async_copy(table_ref, table, sems.at[22])
+    for c in [numbers] + first + later:
         c.start()
-    train_hot = (
-        lax.broadcasted_iota(jnp.int32, (TIDS, count_train), 0) == ids_ref[...]
-    ).astype(jnp.float32)
+    numbers.wait()
+    place = lax.broadcasted_iota(jnp.int32, (TIDS, count_train), 1)
+    ids = jnp.zeros((TIDS, count_train), jnp.int32)
+    for n in range(count_train):
+        ids = jnp.where(place == n, table[2 * HEADS + n], ids)
+    train_hot = (lax.broadcasted_iota(jnp.int32, (TIDS, count_train), 0) == ids).astype(jnp.float32)
     column = lax.broadcasted_iota(jnp.int32, (8 * ROWS, QIDS), 0)
     wanted = jnp.zeros((8 * ROWS, QIDS), jnp.int32)
     for k in range(8):
-        one = query_ids[2 * lax.rem(z + k, 8) + core]
+        one = table[HEADS + 2 * lax.rem(z + k, 8) + core]
         wanted = jnp.where(column // ROWS == k, one, wanted)
     query_hot = (lax.broadcasted_iota(jnp.int32, (8 * ROWS, QIDS), 1) == wanted).astype(jnp.float32)
     row = lax.broadcasted_iota(jnp.int32, (count_train * ROWS, 8 * ROWS), 0)
@@ -170,7 +179,7 @@
         c.wait()
     for e in range(2):
         parity = core if e == 0 else 1 - core
-        fisher = chosen[e].astype(jnp.float32)
+        fisher = fishers[e, table[2 * z + parity]].astype(jnp.float32)
         for k in range(8):
             t = lax.rem(k + 4 * core, 8)
             dy, dx = slot(t // 2 - y), slot(lax.rem(t, 2) * 2 + parity - x)
@@ -199,9 +208,11 @@
 def pair_scores(acts, cots, grads, own_fisher, other_fisher, ids, query_ids, layers):
     count = ids.shape[0]
     bf = jnp.bfloat16
+    table = jnp.concatenate([layers, query_ids, ids])
+    table = jnp.pad(table, (0, 128 - table.shape[0]))
     return pl.pallas_call(
         functools.partial(pair_kernel, count),
-        in_specs=[ANY] * 22 + [VMEM, SMEM, SMEM],
+        in_specs=[ANY] * 19,
         out_specs=VMEM,
         out_shape=jax.ShapeDtypeStruct((TIDS // 2, 4, QIDS), jnp.float32),
         scratch_shapes=[
@@ -209,15 +220,16 @@
             pltpu.VMEM((2, count, HW, HALF), bf),
             pltpu.VMEM((8, HW, HALF), bf),
             pltpu.VMEM((8, SEQ, HALF), bf),
-            pltpu.VMEM((2, HW, HALF), bf),
-            pltpu.SemaphoreType.DMA((22,)),
+            pltpu.VMEM((2,) + own_fisher.shape, bf),
+            pltpu.SMEM((128,), jnp.int32),
+            pltpu.SemaphoreType.DMA((23,)),
         ],
         name="pair_scores",
         compiler_params=pltpu.CompilerParams(vmem_limit_bytes=56 * 2**20),
         cost_estimate=pl.CostEstimate(
             flops=2 * 16 * HW * HALF * SEQ * 4, bytes_accessed=20 * 2**20, transcendentals=0
         ),
-    )(*acts, *cots, *grads, own_fisher, other_fisher, ids.reshape(1, count), query_ids, layers)
+    )(*acts, *cots, *grads, own_fisher, other_fisher, table)
 
 
 def offset_of(y, x):
@@ -260,20 +272,19 @@
     p2 = send(p1, down)
     parts = [unit, send(unit, turn(1, True)), send(unit, turn(-1, True)), send(unit, turn(2, True))]
     other_a = send(own_a, swap)
+    line = stack(*parts)
+    m3 = send(m2, up)
+    p3 = send(p2, down)
+    lp = send(line, turn(1, False))
+    lm = send(line, turn(-1, False))
     own_b = train_grad(train_cotangents, train_inputs, CUTS[0], CUTS[1])
     other_b = send(own_b, swap)
-    la, lb = stack(*parts[:2]), stack(*parts[2:])
-    m3 = send(m2, up)
-    p3 = send(p2, down)
-    lpa, lpb = send(la, turn(1, False)), send(lb, turn(1, False))
-    lma, lmb = send(la, turn(-1, False)), send(lb, turn(-1, False))
+    l2 = send(lp, turn(1, False))
     far = lax.select(core == 0, m3, p3)
     f4 = send(far, lambda y, x, z, c: (y, x, z + 1 - 2 * c, c))
-    l2a = send(lpa, turn(1, False))
-    l2b = send(lmb, turn(-1, False))
     buckets = pair_scores(
         (own_x, p1, p2, p3, f4, m3, m2, m1),
-        (la, lb, lpa, lpb, lma, lmb, l2a, l2b),
+        (line, lp, lm, l2),
         (own_a, own_b, other_a, other_b),
         fisher_diagonal_weight,
         other_fisher,

time: 106 us -> 100 us (0.943)
  Pallas kernels: 22.9 us -> 20.2 us
  starting transfers between devices: 37.6 us -> 35.7 us
  waiting for transfers between devices: 23.9 us -> 22.5 us
  blocking collectives: 19.1 us -> 17.8 us
    pallas_call x2, Pallas kernels: 10.9 us -> 8.82 us  [train_grad(): pl.pallas_call(functools.partial(train_kernel, first, group), in_specs=[A...]
    ppermute x20 -> x17, starting transfers between devices: 37.6 us -> 35.7 us  [send(): lax.ppermute(value, AXES, [(flat(*p), flat(*to(*p))) for p in places])]
    ppermute x20 -> x17, waiting for transfers between devices: 23.9 us -> 22.5 us  [send(): lax.ppermute(value, AXES, [(flat(*p), flat(*to(*p))) for p in places])]
    all_to_all x1, blocking collectives: 19.1 us -> 17.8 us  [local(): lax.all_to_all(buckets, ('y', 'xlo', 'xhi', 'core'), 0, 0, tiled=True)]
  transfers between devices with their start and end apart: 20 -> 17, of which waited for: 10 -> 8; matrix products, arithmetic and copies ran while one was open for 0% -> 1% of each run, Pallas kernels for 5% -> 4%
where the time goes in v2:
time: 100 us
  starting transfers between devices  35.7 us (36%)
  waiting for transfers between devices  22.5 us (22%)
  Pallas kernels  20.2 us (20%)
  blocking collectives  17.8 us (18%)
  local copies, waits for them, and re-layouts  2.31 us (2%)
  other arithmetic  1.43 us (1%)
    ppermute x17, starting transfers between devices, send(): lax.ppermute(value, AXES, [(flat(*p), flat(*to(*p))) for p in places])  35.7 us
    ppermute x17, waiting for transfers between devices, send(): lax.ppermute(value, AXES, [(flat(*p), flat(*to(*p))) for p in places])  22.5 us
    all_to_all x1, blocking collectives, local(): lax.all_to_all(buckets, ('y', 'xlo', 'xhi', 'core'), 0, 0, tiled=True)  17.8 us
    pallas_call x1, Pallas kernels, pair_scores(): pl.pallas_call(functools.partial(pair_kernel, count), in_specs=[ANY] * 19...  11.3 us
    pallas_call x2, Pallas kernels, train_grad(): pl.pallas_call(functools.partial(train_kernel, first, group), in_specs=[A...  8.82 us
  transfers between devices with their start and end apart: 17, of which 8 were waited for; matrix products, arithmetic and copies ran while one was open for 1% of the time, Pallas kernels for 4%

profile of v2, /device:TPU:1, one launch (start us, length us, event | category | flops | bytes accessed | tf_op | source)
XLA Modules:
  0.0 100.2 jit_solution(7943519762568879992)
XLA Ops:
  0.0 0.0 copy-start
  0.0 4.7 %train_grad.3.refs_13_ = bf16[12,240,640]{2,1,0:T(8,128)(2,1)} custom-call(bf16[22,257,240]{2,1,0:T(8,128)(2,1)} %cot_hbm.3, bf16[22,257,640]{2,1,0:T(8,128)(2,1)} %act_hbm.3), custom_call_target="tpu_custom_call" | custom-call | flops 3789619200 | bytes 9114240 | tf_op jit(solution)/shard_map/train_grad/pallas_call | solution.py:73
  4.7 0.0 copy-start.7
  4.7 3.3 %collective-permute-start.15 = (bf16[12,240,640]{2,1,0:T(8,128)(2,1)}, bf16[12,240,640]{2,1,0:T(8,128)(2,1)}, u32[]{:S(2)}, u32[]{:S(2)}) collective-permute-start(bf16[12,240,640]{2,1,0:T(8,128)(2,1)} %train_grad.3.refs_13_), channel_id=1, source_target_pairs={{0,2},{2,0},{4,6},{6,4},{8,10},{10,8},{12,14},{14,12},{16,18},{18,... | collective-permute-start | bytes 11059208 | tf_op jit(solution)/shard_map/ppermute | solution.py:35
  8.0 4.1 %train_grad.2.refs_12_ = bf16[10,240,640]{2,1,0:T(8,128)(2,1)} custom-call(bf16[22,257,240]{2,1,0:T(8,128)(2,1)} %cot_hbm.3, bf16[22,257,640]{2,1,0:T(8,128)(2,1)} %act_hbm.3), custom_call_target="tpu_custom_call" | custom-call | flops 3158016000 | bytes 7595200 | tf_op jit(solution)/shard_map/train_grad/pallas_call | solution.py:73
  12.1 0.1 collective-permute-start.14
  12.3 0.0 copy-done
  12.3 0.1 dynamic-slice_bitcast_fusion.cot_ref
  12.4 0.1 pack.1
  12.5 7.1 %collective-permute-start.7 = (bf16[248,256]{1,0:T(8,128)(2,1)S(1)}, bf16[248,256]{1,0:T(8,128)(2,1)S(1)}, u32[]{:S(2)}, u32[]{:S(2)}) collective-permute-start(bf16[248,256]{1,0:T(8,128)(2,1)S(1)} %pack.1), channel_id=1, source_target_pairs={{0,0},{2,18},{4,4},{6,22},{8,8},{10,26},{12,12},{14,30},{16,16},{1... | collective-permute-start | bytes 380936 | tf_op jit(solution)/shard_map/ppermute | solution.py:35
  19.6 2.6 %collective-permute-done.7.refs_0_ = bf16[248,256]{1,0:T(8,128)(2,1)S(1)} collective-permute-done((bf16[248,256]{1,0:T(8,128)(2,1)S(1)}, bf16[248,256]{1,0:T(8,128)(2,1)S(1)}, u32[]{:S(2)}, u32[]{:S(2)}) %collective-permute-start.7) | collective-permute-done | bytes 127008 | tf_op jit(solution)/shard_map/ppermute | solution.py:35
  22.2 0.0 collective-permute-start.10
  22.2 3.1 %collective-permute-start.9 = (bf16[248,256]{1,0:T(8,128)(2,1)S(1)}, bf16[248,256]{1,0:T(8,128)(2,1)S(1)}, u32[]{:S(2)}, u32[]{:S(2)}) collective-permute-start(bf16[248,256]{1,0:T(8,128)(2,1)S(1)} %collective-permute-done.7.refs_0_), channel_id=1, source_target_pairs={{0,32},{2,66},{4,36},{6,70},{8,40},{10,74},{12,44},{14,78},{16,48}... | collective-permute-start | bytes 380936 | tf_op jit(solution)/shard_map/ppermute | solution.py:35
  25.3 0.0 copy-done.7
  25.3 0.0 collective-permute-start.3
  25.3 2.3 %collective-permute-done.10.refs_3_ = bf16[248,256]{1,0:T(8,128)(2,1)S(1)} collective-permute-done((bf16[248,256]{1,0:T(8,128)(2,1)S(1)}, bf16[248,256]{1,0:T(8,128)(2,1)S(1)}, u32[]{:S(2)}, u32[]{:S(2)}) %collective-permute-start.10) | collective-permute-done | bytes 127008 | tf_op jit(solution)/shard_map/ppermute | solution.py:35
  27.6 4.0 %collective-permute-start = (bf16[257,640]{1,0:T(8,128)(2,1)S(1)}, bf16[257,640]{1,0:T(8,128)(2,1)S(1)}, u32[]{:S(2)}, u32[]{:S(2)}) collective-permute-start(bf16[257,640]{1,0:T(8,128)(2,1)S(1)} %bitcast.8), channel_id=1, source_target_pairs={{0,28},{2,30},{4,0},{6,2},{8,4},{10,6},{12,8},{14,10},{16,12},{18,... | collective-permute-start | bytes 986888 | tf_op jit(solution)/shard_map/ppermute | solution.py:35
  31.6 0.0 collective-permute-done.9.refs_2_
  31.6 0.7 collective-permute-start.8
  32.3 3.4 %collective-permute-done.8.refs_1_ = bf16[248,256]{1,0:T(8,128)(2,1)S(1)} collective-permute-done((bf16[248,256]{1,0:T(8,128)(2,1)S(1)}, bf16[248,256]{1,0:T(8,128)(2,1)S(1)}, u32[]{:S(2)}, u32[]{:S(2)}) %collective-permute-start.8) | collective-permute-done | bytes 127008 | tf_op jit(solution)/shard_map/ppermute | solution.py:35
  35.7 0.0 copy-start.1
  35.7 2.1 %collective-permute-start.11 = (bf16[4,248,256]{2,1,0:T(8,128)(2,1)S(1)}, bf16[4,248,256]{2,1,0:T(8,128)(2,1)S(1)}, u32[]{:S(2)}, u32[]{:S(2)}) collective-permute-start(bf16[4,248,256]{2,1,0:T(8,128)(2,1)S(1)} %stack.1.refs_8_), channel_id=1, source_target_pairs={{0,192},{2,35},{4,196},{6,39},{8,200},{10,43},{12,204},{14,47},{16... | collective-permute-start | bytes 1523720 | tf_op jit(solution)/shard_map/ppermute | solution.py:35
  37.8 0.0 collective-permute-done.3.refs_7_
  37.8 0.0 copy-start.8
  37.8 0.2 collective-permute-start.4
  38.0 1.0 collective-permute-done.refs_1_
  39.0 0.0 copy-start.9
  39.0 3.1 %collective-permute-start.1 = (bf16[257,640]{1,0:T(8,128)(2,1)S(1)}, bf16[257,640]{1,0:T(8,128)(2,1)S(1)}, u32[]{:S(2)}, u32[]{:S(2)}) collective-permute-start(bf16[257,640]{1,0:T(8,128)(2,1)S(1)} %collective-permute-done.refs_1_), channel_id=1, source_target_pairs={{0,28},{2,30},{4,0},{6,2},{8,4},{10,6},{12,8},{14,10},{16,12},{18,... | collective-permute-start | bytes 986888 | tf_op jit(solution)/shard_map/ppermute | solution.py:35
  42.1 3.8 %collective-permute-done.4.refs_6_ = bf16[257,640]{1,0:T(8,128)(2,1)} collective-permute-done((bf16[257,640]{1,0:T(8,128)(2,1)S(1)}, bf16[257,640]{1,0:T(8,128)(2,1)}, u32[]{:S(2)}, u32[]{:S(2)}) %collective-permute-start.4) | collective-permute-done | bytes 328992 | tf_op jit(solution)/shard_map/ppermute | solution.py:35
  45.9 3.7 %collective-permute-start.16 = (bf16[2,240,640]{2,1,0:T(8,128)(2,1)}, bf16[2,240,640]{2,1,0:T(8,128)(2,1)}, u32[]{:S(2)}, u32[]{:S(2)}) collective-permute-start(bf16[2,240,640]{2,1,0:T(8,128)(2,1)} %refs_16_.1), channel_id=1, source_target_pairs={{0,2},{2,0},{4,6},{6,4},{8,10},{10,8},{12,14},{14,12},{16,18},{18,... | collective-permute-start | bytes 1843208 | tf_op jit(solution)/shard_map/ppermute | solution.py:35
  49.6 0.0 copy-done.8
  49.6 0.0 collective-permute-done.1.refs_2_
  49.6 0.0 copy-start.10
  49.6 0.3 collective-permute-start.5
  49.8 0.0 copy-done.9
  49.9 0.0 collective-permute-done.11.refs_9_
  49.9 0.0 copy-start.4
  49.9 0.8 copy-done.4
  50.6 2.6 %collective-permute-start.2 = (bf16[257,640]{1,0:T(8,128)(2,1)S(1)}, bf16[257,640]{1,0:T(8,128)(2,1)S(1)}, u32[]{:S(2)}, u32[]{:S(2)}) collective-permute-start(bf16[257,640]{1,0:T(8,128)(2,1)S(1)} %collective-permute-done.1.refs_2_), channel_id=1, source_target_pairs={{0,28},{2,30},{4,0},{6,2},{8,4},{10,6},{12,8},{14,10},{16,12},{18,... | collective-permute-start | bytes 986888 | tf_op jit(solution)/shard_map/ppermute | solution.py:35
  53.3 6.6 %collective-permute-done.5.refs_5_ = bf16[257,640]{1,0:T(8,128)(2,1)S(1)} collective-permute-done((bf16[257,640]{1,0:T(8,128)(2,1)}, bf16[257,640]{1,0:T(8,128)(2,1)S(1)}, u32[]{:S(2)}, u32[]{:S(2)}) %collective-permute-start.5) | collective-permute-done | bytes 328992 | tf_op jit(solution)/shard_map/ppermute | solution.py:35
  59.9 0.0 copy-start.2
  59.9 1.3 %collective-permute-start.12 = (bf16[4,248,256]{2,1,0:T(8,128)(2,1)S(1)}, bf16[4,248,256]{2,1,0:T(8,128)(2,1)S(1)}, u32[]{:S(2)}, u32[]{:S(2)}) collective-permute-start(bf16[4,248,256]{2,1,0:T(8,128)(2,1)S(1)} %stack.1.refs_8_), channel_id=1, source_target_pairs={{0,64},{2,34},{4,68},{6,38},{8,72},{10,42},{12,76},{14,46},{16,80}... | collective-permute-start | bytes 1523720 | tf_op jit(solution)/shard_map/ppermute | solution.py:35
  61.2 0.0 collective-permute-done.2.refs_3_
  61.2 0.0 copy-start.3
  61.2 1.4 %collective-permute-start.13 = (bf16[4,248,256]{2,1,0:T(8,128)(2,1)}, bf16[4,248,256]{2,1,0:T(8,128)(2,1)S(1)}, u32[]{:S(2)}, u32[]{:S(2)}) collective-permute-start(bf16[4,248,256]{2,1,0:T(8,128)(2,1)} %copy-done.4), channel_id=1, source_target_pairs={{0,192},{2,35},{4,196},{6,39},{8,200},{10,43},{12,204},{14,47},{16... | collective-permute-start | bytes 1523720 | tf_op jit(solution)/shard_map/ppermute | solution.py:35
  62.6 0.0 collective-permute-done.16.refs_17_
  62.6 2.8 %collective-permute-start.6 = (bf16[257,640]{1,0:T(8,128)(2,1)S(1)}, bf16[257,640]{1,0:T(8,128)(2,1)S(1)}, u32[]{:S(2)}, u32[]{:S(2)}) collective-permute-start(bf16[257,640]{1,0:T(8,128)(2,1)S(1)} %broadcast_select_fusion), channel_id=1, source_target_pairs={{0,4},{2,30},{4,8},{6,2},{8,12},{10,6},{12,16},{14,10},{16,20},{18... | collective-permute-start | bytes 986888 | tf_op jit(solution)/shard_map/ppermute | solution.py:35
  65.4 0.8 pad_add_fusion
  66.2 0.5 pad.4.refs_18_
  66.7 2.5 %collective-permute-done.12.refs_10_ = bf16[4,248,256]{2,1,0:T(8,128)(2,1)S(1)} collective-permute-done((bf16[4,248,256]{2,1,0:T(8,128)(2,1)S(1)}, bf16[4,248,256]{2,1,0:T(8,128)(2,1)S(1)}, u32[]{:S(2)}, u32[]{:S(2)}) %collective-permute-start.12) | collective-permute-done | bytes 507936 | tf_op jit(solution)/shard_map/ppermute | solution.py:35
  69.2 0.3 collective-permute-done.13.refs_11_
  69.6 0.0 collective-permute-done.6.refs_4_
  69.6 0.0 collective-permute-done.14.refs_14_
  69.6 0.0 collective-permute-done.15.refs_15_
  69.6 0.0 copy-done.1
  69.6 0.0 copy-done.10
  69.6 0.0 copy-done.2
  69.6 0.0 copy-done.3
  69.6 0.4 copy-done.5
  70.0 0.3 copy-done.6
  70.3 0.1 copy-done.11
  70.5 11.3 %pair_scores.1 = f32[32,4,16]{2,1,0:T(4,128)} custom-call(bf16[257,640]{1,0:T(8,128)(2,1)} %bitcast.6, bf16[257,640]{1,0:T(8,128)(2,1)} %copy-done.9, bf16[257,640]{1,0:T(8,128)(2,1)} %copy-done.10, bf16[257,640]{1,0:T(8,128)(2,1)} %copy-done.3, bf16[257,640]{1,0:T(8,128)(2,1)} %copy-done.11, bf16[257,640]{1,0:T(8,128)(2,1)} %copy-done.2, ...), custom_call_target="tpu_custom_call" | custom-call | flops 5052825600 | bytes 20971520 | tf_op jit(solution)/shard_map/pair_scores/pallas_call | solution.py:213
  81.8 17.8 %all_to_all.5 = f32[32,4,16]{2,1,0:T(4,128)S(1)} all-to-all(f32[32,4,16]{2,1,0:T(4,128)} %pair_scores.1), channel_id=1, replica_groups=mesh['y'=4,'xlo'=2,'z'=8,'core'=2,'xhi'=2] {'y','xlo','xhi','core'}, dimensions={0} | all-to-all | bytes 16384 | tf_op jit(solution)/shard_map/all_to_all | solution.py:295
  99.6 0.6 reduce_sum.9
  (5 shorter events, 0.1 us)
Async XLA Ops:
  0.0 12.3 %copy-start = (bf16[1,257,3840]{2,1,0:T(8,128)(2,1)S(1)}, bf16[1,257,3840]{2,1,0:T(8,128)(2,1)}, u32[]{:S(2)}) copy-start(bf16[1,257,3840]{2,1,0:T(8,128)(2,1)} %param.12) | copy-start | bytes 5921284
  4.7 20.6 %copy-start.7 = (bf16[1,257,640]{2,1,0:T(8,128)(2,1)S(1)}, bf16[1,257,640]{2,1,0:T(8,128)(2,1)}, u32[]{:S(2)}) copy-start(bf16[1,257,640]{2,1,0:T(8,128)(2,1)} %param.11) | copy-start | bytes 986884
  4.7 64.9 %collective-permute-start.15 = (bf16[12,240,640]{2,1,0:T(8,128)(2,1)}, bf16[12,240,640]{2,1,0:T(8,128)(2,1)}, u32[]{:S(2)}, u32[]{:S(2)}) collective-permute-start(bf16[12,240,640]{2,1,0:T(8,128)(2,1)} %train_grad.3.refs_13_), channel_id=1, source_target_pairs={{0,2},{2,0},{4,6},{6,4},{8,10},{10,8},{12,14},{14,12},{16,18},{18,... | collective-permute-start | bytes 11059208 | tf_op jit(solution)/shard_map/ppermute | solution.py:35
  12.1 57.4 %collective-permute-start.14 = (bf16[10,240,640]{2,1,0:T(8,128)(2,1)}, bf16[10,240,640]{2,1,0:T(8,128)(2,1)}, u32[]{:S(2)}, u32[]{:S(2)}) collective-permute-start(bf16[10,240,640]{2,1,0:T(8,128)(2,1)} %train_grad.2.refs_12_), channel_id=1, source_target_pairs={{0,2},{2,0},{4,6},{6,4},{8,10},{10,8},{12,14},{14,12},{16,18},{18,... | collective-permute-start | bytes 9216008 | tf_op jit(solution)/shard_map/ppermute | solution.py:35
  12.5 9.7 %collective-permute-start.7 = (bf16[248,256]{1,0:T(8,128)(2,1)S(1)}, bf16[248,256]{1,0:T(8,128)(2,1)S(1)}, u32[]{:S(2)}, u32[]{:S(2)}) collective-permute-start(bf16[248,256]{1,0:T(8,128)(2,1)S(1)} %pack.1), channel_id=1, source_target_pairs={{0,0},{2,18},{4,4},{6,22},{8,8},{10,26},{12,12},{14,30},{16,16},{1... | collective-permute-start | bytes 380936 | tf_op jit(solution)/shard_map/ppermute | solution.py:35
  22.2 5.4 %collective-permute-start.10 = (bf16[248,256]{1,0:T(8,128)(2,1)S(1)}, bf16[248,256]{1,0:T(8,128)(2,1)S(1)}, u32[]{:S(2)}, u32[]{:S(2)}) collective-permute-start(bf16[248,256]{1,0:T(8,128)(2,1)S(1)} %collective-permute-done.7.refs_0_), channel_id=1, source_target_pairs={{0,1},{2,130},{4,5},{6,134},{8,9},{10,138},{12,13},{14,142},{16,17... | collective-permute-start | bytes 380936 | tf_op jit(solution)/shard_map/ppermute | solution.py:35
  22.2 9.4 %collective-permute-start.9 = (bf16[248,256]{1,0:T(8,128)(2,1)S(1)}, bf16[248,256]{1,0:T(8,128)(2,1)S(1)}, u32[]{:S(2)}, u32[]{:S(2)}) collective-permute-start(bf16[248,256]{1,0:T(8,128)(2,1)S(1)} %collective-permute-done.7.refs_0_), channel_id=1, source_target_pairs={{0,32},{2,66},{4,36},{6,70},{8,40},{10,74},{12,44},{14,78},{16,48}... | collective-permute-start | bytes 380936 | tf_op jit(solution)/shard_map/ppermute | solution.py:35
  25.3 12.5 %collective-permute-start.3 = (bf16[257,640]{1,0:T(8,128)(2,1)S(1)}, bf16[257,640]{1,0:T(8,128)(2,1)S(1)}, u32[]{:S(2)}, u32[]{:S(2)}) collective-permute-start(bf16[257,640]{1,0:T(8,128)(2,1)S(1)} %bitcast.7), channel_id=1, source_target_pairs={{0,4},{2,6},{4,8},{6,10},{8,12},{10,14},{12,16},{14,18},{16,20},{1... | collective-permute-start | bytes 986888 | tf_op jit(solution)/shard_map/ppermute | solution.py:35
  27.6 11.4 %collective-permute-start = (bf16[257,640]{1,0:T(8,128)(2,1)S(1)}, bf16[257,640]{1,0:T(8,128)(2,1)S(1)}, u32[]{:S(2)}, u32[]{:S(2)}) collective-permute-start(bf16[257,640]{1,0:T(8,128)(2,1)S(1)} %bitcast.8), channel_id=1, source_target_pairs={{0,28},{2,30},{4,0},{6,2},{8,4},{10,6},{12,8},{14,10},{16,12},{18,... | collective-permute-start | bytes 986888 | tf_op jit(solution)/shard_map/ppermute | solution.py:35
  31.6 4.1 %collective-permute-start.8 = (bf16[248,256]{1,0:T(8,128)(2,1)S(1)}, bf16[248,256]{1,0:T(8,128)(2,1)S(1)}, u32[]{:S(2)}, u32[]{:S(2)}) collective-permute-start(bf16[248,256]{1,0:T(8,128)(2,1)S(1)} %collective-permute-done.7.refs_0_), channel_id=1, source_target_pairs={{0,33},{2,194},{4,37},{6,198},{8,41},{10,202},{12,45},{14,206},{16... | collective-permute-start | bytes 380936 | tf_op jit(solution)/shard_map/ppermute | solution.py:35
  35.7 33.8 %copy-start.1 = (bf16[4,248,256]{2,1,0:T(8,128)(2,1)}, bf16[4,248,256]{2,1,0:T(8,128)(2,1)S(1)}, u32[]{:S(2)}) copy-start(bf16[4,248,256]{2,1,0:T(8,128)(2,1)S(1)} %stack.1.refs_8_) | copy-start | bytes 1523716
  35.7 14.1 %collective-permute-start.11 = (bf16[4,248,256]{2,1,0:T(8,128)(2,1)S(1)}, bf16[4,248,256]{2,1,0:T(8,128)(2,1)S(1)}, u32[]{:S(2)}, u32[]{:S(2)}) collective-permute-start(bf16[4,248,256]{2,1,0:T(8,128)(2,1)S(1)} %stack.1.refs_8_), channel_id=1, source_target_pairs={{0,192},{2,35},{4,196},{6,39},{8,200},{10,43},{12,204},{14,47},{16... | collective-permute-start | bytes 1523720 | tf_op jit(solution)/shard_map/ppermute | solution.py:35
  37.8 11.8 %copy-start.8 = (bf16[257,640]{1,0:T(8,128)(2,1)}, bf16[257,640]{1,0:T(8,128)(2,1)S(1)}, u32[]{:S(2)}) copy-start(bf16[257,640]{1,0:T(8,128)(2,1)S(1)} %collective-permute-done.3.refs_7_) | copy-start | bytes 986884
  37.8 8.1 %collective-permute-start.4 = (bf16[257,640]{1,0:T(8,128)(2,1)S(1)}, bf16[257,640]{1,0:T(8,128)(2,1)}, u32[]{:S(2)}, u32[]{:S(2)}) collective-permute-start(bf16[257,640]{1,0:T(8,128)(2,1)S(1)} %collective-permute-done.3.refs_7_), channel_id=1, source_target_pairs={{0,4},{2,6},{4,8},{6,10},{8,12},{10,14},{12,16},{14,18},{16,20},{1... | collective-permute-start | bytes 986888 | tf_op jit(solution)/shard_map/ppermute | solution.py:35
  39.0 10.9 %copy-start.9 = (bf16[257,640]{1,0:T(8,128)(2,1)}, bf16[257,640]{1,0:T(8,128)(2,1)S(1)}, u32[]{:S(2)}) copy-start(bf16[257,640]{1,0:T(8,128)(2,1)S(1)} %collective-permute-done.refs_1_) | copy-start | bytes 986884
  39.0 10.6 %collective-permute-start.1 = (bf16[257,640]{1,0:T(8,128)(2,1)S(1)}, bf16[257,640]{1,0:T(8,128)(2,1)S(1)}, u32[]{:S(2)}, u32[]{:S(2)}) collective-permute-start(bf16[257,640]{1,0:T(8,128)(2,1)S(1)} %collective-permute-done.refs_1_), channel_id=1, source_target_pairs={{0,28},{2,30},{4,0},{6,2},{8,4},{10,6},{12,8},{14,10},{16,12},{18,... | collective-permute-start | bytes 986888 | tf_op jit(solution)/shard_map/ppermute | solution.py:35
  45.9 16.7 %collective-permute-start.16 = (bf16[2,240,640]{2,1,0:T(8,128)(2,1)}, bf16[2,240,640]{2,1,0:T(8,128)(2,1)}, u32[]{:S(2)}, u32[]{:S(2)}) collective-permute-start(bf16[2,240,640]{2,1,0:T(8,128)(2,1)} %refs_16_.1), channel_id=1, source_target_pairs={{0,2},{2,0},{4,6},{6,4},{8,10},{10,8},{12,14},{14,12},{16,18},{18,... | collective-permute-start | bytes 1843208 | tf_op jit(solution)/shard_map/ppermute | solution.py:35
  49.6 20.0 %copy-start.10 = (bf16[257,640]{1,0:T(8,128)(2,1)}, bf16[257,640]{1,0:T(8,128)(2,1)S(1)}, u32[]{:S(2)}) copy-start(bf16[257,640]{1,0:T(8,128)(2,1)S(1)} %collective-permute-done.1.refs_2_) | copy-start | bytes 986884
  49.6 10.3 %collective-permute-start.5 = (bf16[257,640]{1,0:T(8,128)(2,1)}, bf16[257,640]{1,0:T(8,128)(2,1)S(1)}, u32[]{:S(2)}, u32[]{:S(2)}) collective-permute-start(bf16[257,640]{1,0:T(8,128)(2,1)} %collective-permute-done.4.refs_6_), channel_id=1, source_target_pairs={{0,4},{2,6},{4,8},{6,10},{8,12},{10,14},{12,16},{14,18},{16,20},{1... | collective-permute-start | bytes 986888 | tf_op jit(solution)/shard_map/ppermute | solution.py:35
  49.9 0.8 copy-start.4
  50.6 10.5 %collective-permute-start.2 = (bf16[257,640]{1,0:T(8,128)(2,1)S(1)}, bf16[257,640]{1,0:T(8,128)(2,1)S(1)}, u32[]{:S(2)}, u32[]{:S(2)}) collective-permute-start(bf16[257,640]{1,0:T(8,128)(2,1)S(1)} %collective-permute-done.1.refs_2_), channel_id=1, source_target_pairs={{0,28},{2,30},{4,0},{6,2},{8,4},{10,6},{12,8},{14,10},{16,12},{18,... | collective-permute-start | bytes 986888 | tf_op jit(solution)/shard_map/ppermute | solution.py:35
  59.9 9.7 %copy-start.2 = (bf16[257,640]{1,0:T(8,128)(2,1)}, bf16[257,640]{1,0:T(8,128)(2,1)S(1)}, u32[]{:S(2)}) copy-start(bf16[257,640]{1,0:T(8,128)(2,1)S(1)} %collective-permute-done.5.refs_5_) | copy-start | bytes 986884
  59.9 9.4 %collective-permute-start.12 = (bf16[4,248,256]{2,1,0:T(8,128)(2,1)S(1)}, bf16[4,248,256]{2,1,0:T(8,128)(2,1)S(1)}, u32[]{:S(2)}, u32[]{:S(2)}) collective-permute-start(bf16[4,248,256]{2,1,0:T(8,128)(2,1)S(1)} %stack.1.refs_8_), channel_id=1, source_target_pairs={{0,64},{2,34},{4,68},{6,38},{8,72},{10,42},{12,76},{14,46},{16,80}... | collective-permute-start | bytes 1523720 | tf_op jit(solution)/shard_map/ppermute | solution.py:35
  61.2 8.4 %copy-start.3 = (bf16[257,640]{1,0:T(8,128)(2,1)}, bf16[257,640]{1,0:T(8,128)(2,1)S(1)}, u32[]{:S(2)}) copy-start(bf16[257,640]{1,0:T(8,128)(2,1)S(1)} %collective-permute-done.2.refs_3_) | copy-start | bytes 986884
  61.2 8.4 %collective-permute-start.13 = (bf16[4,248,256]{2,1,0:T(8,128)(2,1)}, bf16[4,248,256]{2,1,0:T(8,128)(2,1)S(1)}, u32[]{:S(2)}, u32[]{:S(2)}) collective-permute-start(bf16[4,248,256]{2,1,0:T(8,128)(2,1)} %copy-done.4), channel_id=1, source_target_pairs={{0,192},{2,35},{4,196},{6,39},{8,200},{10,43},{12,204},{14,47},{16... | collective-permute-start | bytes 1523720 | tf_op jit(solution)/shard_map/ppermute | solution.py:35
  62.6 7.0 %collective-permute-start.6 = (bf16[257,640]{1,0:T(8,128)(2,1)S(1)}, bf16[257,640]{1,0:T(8,128)(2,1)S(1)}, u32[]{:S(2)}, u32[]{:S(2)}) collective-permute-start(bf16[257,640]{1,0:T(8,128)(2,1)S(1)} %broadcast_select_fusion), channel_id=1, source_target_pairs={{0,4},{2,30},{4,8},{6,2},{8,12},{10,6},{12,16},{14,10},{16,20},{18... | collective-permute-start | bytes 986888 | tf_op jit(solution)/shard_map/ppermute | solution.py:35
  69.2 0.8 copy-start.5
  69.6 0.8 copy-start.6
  69.6 0.9 copy-start.11

commit v3 on v2

--- a/solution.py
+++ b/solution.py
@@ -18,7 +18,7 @@
 HW = 3 * HEAD_DIM
 HALF = D // 2
 ROWS = 16
-CUTS = (10, 12)
+CUTS = (8, 6, 8)
 NY, NXL, NZ, NC, NXH = 4, 2, 8, 2, 2
 AXES = ("y", "xlo", "z", "core", "xhi")
 SCALE = 1.0 / (SEQ * math.sqrt(HW * D))
@@ -136,7 +136,7 @@
 def pair_kernel(count_train, *refs):
     acts, refs = refs[:8], refs[8:]
     cots, refs = refs[:4], refs[4:]
-    grads, refs = refs[:4], refs[4:]
+    grads, refs = refs[:6], refs[6:]
     own_fisher, other_fisher, table_ref, out_ref = refs[:4]
     cot, grad, weighted, act, fishers, table, sems = refs[4:]
     core, z, y = lax.axis_index("core"), lax.axis_index("z"), lax.axis_index("y")
@@ -150,9 +150,9 @@
         first.append(pltpu.make_async_copy(ref, fishers.at[e], sems.at[16 + e]))
     later = []
     for i, ref in enumerate(grads):
-        e, rows = i // 2, pl.ds((i % 2) * CUTS[0], ref.shape[0])
+        e, rows = i // 3, pl.ds(sum(CUTS[: i % 3]), ref.shape[0])
         later.append(pltpu.make_async_copy(ref, grad.at[e, rows], sems.at[18 + i]))
-    numbers = pltpu.make_async_copy(table_ref, table, sems.at[22])
+    numbers = pltpu.make_async_copy(table_ref, table, sems.at[24])
     for c in [numbers] + first + later:
         c.start()
     numbers.wait()
@@ -185,7 +185,7 @@
             dy, dx = slot(t // 2 - y), slot(lax.rem(t, 2) * 2 + parity - x)
             unit = jnp.where(core == 0, dy * 4 + dx, dx * 4 + dy)
             weighted[k] = (fisher * turned_sum(cot[unit], act[k])).astype(jnp.bfloat16)
-        for c in later[2 * e : 2 * e + 2]:
+        for c in later[3 * e : 3 * e + 3]:
             c.wait()
         total = jnp.zeros((count_train * ROWS, 8 * ROWS), jnp.float32)
         for r in range(0, HW, ROWS):
@@ -212,7 +212,7 @@
     table = jnp.pad(table, (0, 128 - table.shape[0]))
     return pl.pallas_call(
         functools.partial(pair_kernel, count),
-        in_specs=[ANY] * 19,
+        in_specs=[ANY] * 21,
         out_specs=VMEM,
         out_shape=jax.ShapeDtypeStruct((TIDS // 2, 4, QIDS), jnp.float32),
         scratch_shapes=[
@@ -222,7 +222,7 @@
             pltpu.VMEM((8, SEQ, HALF), bf),
             pltpu.VMEM((2,) + own_fisher.shape, bf),
             pltpu.SMEM((128,), jnp.int32),
-            pltpu.SemaphoreType.DMA((23,)),
+            pltpu.SemaphoreType.DMA((25,)),
         ],
         name="pair_scores",
         compiler_params=pltpu.CompilerParams(vmem_limit_bytes=56 * 2**20),
@@ -280,12 +280,14 @@
     own_b = train_grad(train_cotangents, train_inputs, CUTS[0], CUTS[1])
     other_b = send(own_b, swap)
     l2 = send(lp, turn(1, False))
+    own_c = train_grad(train_cotangents, train_inputs, CUTS[0] + CUTS[1], CUTS[2])
+    other_c = send(own_c, swap)
     far = lax.select(core == 0, m3, p3)
     f4 = send(far, lambda y, x, z, c: (y, x, z + 1 - 2 * c, c))
     buckets = pair_scores(
         (own_x, p1, p2, p3, f4, m3, m2, m1),
         (line, lp, lm, l2),
-        (own_a, own_b, other_a, other_b),
+        (own_a, own_b, own_c, other_a, other_b, other_c),
         fisher_diagonal_weight,
         other_fisher,
         train_ids,

time: 100 us -> 108 us (1.080)
  waiting for transfers between devices: 22.5 us -> 34 us
  starting transfers between devices: 35.7 us -> 30.2 us
  Pallas kernels: 20.2 us -> 22.2 us
  blocking collectives: 17.8 us -> 19 us
    ppermute x17 -> x18, waiting for transfers between devices: 22.5 us -> 34 us  [send(): lax.ppermute(value, AXES, [(flat(*p), flat(*to(*p))) for p in places])]
    ppermute x17 -> x18, starting transfers between devices: 35.7 us -> 30.2 us  [send(): lax.ppermute(value, AXES, [(flat(*p), flat(*to(*p))) for p in places])]
    pallas_call x2 -> x3, Pallas kernels: 8.82 us -> 10.8 us  [train_grad(): pl.pallas_call(functools.partial(train_kernel, first, group), in_specs=[A...]
    all_to_all x1, blocking collectives: 17.8 us -> 19 us  [local(): lax.all_to_all(buckets, ('y', 'xlo', 'xhi', 'core'), 0, 0, tiled=True)]
  transfers between devices with their start and end apart: 17 -> 18, of which waited for: 8 -> 11; matrix products, arithmetic and copies ran while one was open for 1% -> 1% of each run, Pallas kernels for 4% -> 7%
where the time goes in v3:
time: 108 us
  waiting for transfers between devices  34 us (31%)
  starting transfers between devices  30.2 us (28%)
  Pallas kernels  22.2 us (21%)
  blocking collectives  19 us (18%)
  local copies, waits for them, and re-layouts  1.37 us (1%)
    ppermute x18, waiting for transfers between devices, send(): lax.ppermute(value, AXES, [(flat(*p), flat(*to(*p))) for p in places])  34 us
    ppermute x18, starting transfers between devices, send(): lax.ppermute(value, AXES, [(flat(*p), flat(*to(*p))) for p in places])  30.2 us
    all_to_all x1, blocking collectives, local(): lax.all_to_all(buckets, ('y', 'xlo', 'xhi', 'core'), 0, 0, tiled=True)  19 us
    pallas_call x1, Pallas kernels, pair_scores(): pl.pallas_call(functools.partial(pair_kernel, count), in_specs=[ANY] * 21...  11.3 us
    pallas_call x3, Pallas kernels, train_grad(): pl.pallas_call(functools.partial(train_kernel, first, group), in_specs=[A...  10.8 us
  transfers between devices with their start and end apart: 18, of which 11 were waited for; matrix products, arithmetic and copies ran while one was open for 1% of the time, Pallas kernels for 7%

profile of v3, /device:TPU:1, one launch (start us, length us, event | category | flops | bytes accessed | tf_op | source)
XLA Modules:
  0.0 107.8 jit_solution(11742697218995775891)
XLA Ops:
  0.0 0.0 copy-start
  0.0 3.8 %train_grad.5.refs_14_ = bf16[8,240,640]{2,1,0:T(8,128)(2,1)} custom-call(bf16[22,257,240]{2,1,0:T(8,128)(2,1)} %cot_hbm.5, bf16[22,257,640]{2,1,0:T(8,128)(2,1)} %act_hbm.5), custom_call_target="tpu_custom_call" | custom-call | flops 2526412800 | bytes 6076160 | tf_op jit(solution)/shard_map/train_grad/pallas_call | solution.py:73
  3.9 0.0 copy-start.8
  3.9 0.0 copy-start.4
  3.9 3.3 %collective-permute-start.16 = (bf16[8,240,640]{2,1,0:T(8,128)(2,1)}, bf16[8,240,640]{2,1,0:T(8,128)(2,1)}, u32[]{:S(2)}, u32[]{:S(2)}) collective-permute-start(bf16[8,240,640]{2,1,0:T(8,128)(2,1)} %train_grad.5.refs_14_), channel_id=1, source_target_pairs={{0,2},{2,0},{4,6},{6,4},{8,10},{10,8},{12,14},{14,12},{16,18},{18,... | collective-permute-start | bytes 7372808 | tf_op jit(solution)/shard_map/ppermute | solution.py:35
  7.2 3.7 %train_grad.3.refs_12_ = bf16[8,240,640]{2,1,0:T(8,128)(2,1)} custom-call(bf16[22,257,240]{2,1,0:T(8,128)(2,1)} %cot_hbm.5, bf16[22,257,640]{2,1,0:T(8,128)(2,1)} %act_hbm.5), custom_call_target="tpu_custom_call" | custom-call | flops 2526412800 | bytes 6076160 | tf_op jit(solution)/shard_map/train_grad/pallas_call | solution.py:73
  10.9 0.2 collective-permute-start.14
  11.0 0.0 copy-done
  11.0 0.1 dynamic-slice_bitcast_fusion.cot_ref
  11.2 0.1 pack.1
  11.2 7.1 %collective-permute-start.7 = (bf16[248,256]{1,0:T(8,128)(2,1)S(1)}, bf16[248,256]{1,0:T(8,128)(2,1)S(1)}, u32[]{:S(2)}, u32[]{:S(2)}) collective-permute-start(bf16[248,256]{1,0:T(8,128)(2,1)S(1)} %pack.1), channel_id=1, source_target_pairs={{0,0},{2,18},{4,4},{6,22},{8,8},{10,26},{12,12},{14,30},{16,16},{1... | collective-permute-start | bytes 380936 | tf_op jit(solution)/shard_map/ppermute | solution.py:35
  18.4 2.6 %collective-permute-done.7.refs_0_ = bf16[248,256]{1,0:T(8,128)(2,1)S(1)} collective-permute-done((bf16[248,256]{1,0:T(8,128)(2,1)S(1)}, bf16[248,256]{1,0:T(8,128)(2,1)S(1)}, u32[]{:S(2)}, u32[]{:S(2)}) %collective-permute-start.7) | collective-permute-done | bytes 127008 | tf_op jit(solution)/shard_map/ppermute | solution.py:35
  20.9 0.0 collective-permute-start.10
  20.9 3.1 %collective-permute-start.9 = (bf16[248,256]{1,0:T(8,128)(2,1)S(1)}, bf16[248,256]{1,0:T(8,128)(2,1)S(1)}, u32[]{:S(2)}, u32[]{:S(2)}) collective-permute-start(bf16[248,256]{1,0:T(8,128)(2,1)S(1)} %collective-permute-done.7.refs_0_), channel_id=1, source_target_pairs={{0,32},{2,66},{4,36},{6,70},{8,40},{10,74},{12,44},{14,78},{16,48}... | collective-permute-start | bytes 380936 | tf_op jit(solution)/shard_map/ppermute | solution.py:35
  24.0 0.0 collective-permute-start.8
  24.0 2.3 %collective-permute-done.10.refs_3_ = bf16[248,256]{1,0:T(8,128)(2,1)S(1)} collective-permute-done((bf16[248,256]{1,0:T(8,128)(2,1)S(1)}, bf16[248,256]{1,0:T(8,128)(2,1)S(1)}, u32[]{:S(2)}, u32[]{:S(2)}) %collective-permute-start.10) | collective-permute-done | bytes 127008 | tf_op jit(solution)/shard_map/ppermute | solution.py:35
  26.3 0.0 copy-done.8
  26.3 0.5 collective-permute-start.3
  26.8 0.5 collective-permute-done.9.refs_2_
  27.3 0.0 copy-done.4
  27.3 2.1 %collective-permute-start.17 = (bf16[2,240,640]{2,1,0:T(8,128)(2,1)S(1)}, bf16[2,240,640]{2,1,0:T(8,128)(2,1)S(1)}, u32[]{:S(2)}, u32[]{:S(2)}) collective-permute-start(bf16[2,240,640]{2,1,0:T(8,128)(2,1)S(1)} %copy-done.4), channel_id=1, source_target_pairs={{0,2},{2,0},{4,6},{6,4},{8,10},{10,8},{12,14},{14,12},{16,18},{18,... | collective-permute-start | bytes 1843208 | tf_op jit(solution)/shard_map/ppermute | solution.py:35
  29.4 0.0 collective-permute-done.8.refs_1_
  29.4 3.4 %collective-permute-start = (bf16[257,640]{1,0:T(8,128)(2,1)S(1)}, bf16[257,640]{1,0:T(8,128)(2,1)S(1)}, u32[]{:S(2)}, u32[]{:S(2)}) collective-permute-start(bf16[257,640]{1,0:T(8,128)(2,1)S(1)} %bitcast.8), channel_id=1, source_target_pairs={{0,28},{2,30},{4,0},{6,2},{8,4},{10,6},{12,8},{14,10},{16,12},{18,... | collective-permute-start | bytes 986888 | tf_op jit(solution)/shard_map/ppermute | solution.py:35
  32.7 3.3 %train_grad.4.refs_13_ = bf16[6,240,640]{2,1,0:T(8,128)(2,1)} custom-call(bf16[22,257,240]{2,1,0:T(8,128)(2,1)} %cot_hbm.5, bf16[22,257,640]{2,1,0:T(8,128)(2,1)} %act_hbm.5), custom_call_target="tpu_custom_call" | custom-call | flops 1894809600 | bytes 4557120 | tf_op jit(solution)/shard_map/train_grad/pallas_call | solution.py:73
  36.0 2.3 %collective-permute-done.3.refs_7_ = bf16[257,640]{1,0:T(8,128)(2,1)S(1)} collective-permute-done((bf16[257,640]{1,0:T(8,128)(2,1)S(1)}, bf16[257,640]{1,0:T(8,128)(2,1)S(1)}, u32[]{:S(2)}, u32[]{:S(2)}) %collective-permute-start.3) | collective-permute-done | bytes 328992 | tf_op jit(solution)/shard_map/ppermute | solution.py:35
  38.3 0.4 collective-permute-start.15
  38.7 1.3 %collective-permute-done.refs_1_ = bf16[257,640]{1,0:T(8,128)(2,1)S(1)} collective-permute-done((bf16[257,640]{1,0:T(8,128)(2,1)S(1)}, bf16[257,640]{1,0:T(8,128)(2,1)S(1)}, u32[]{:S(2)}, u32[]{:S(2)}) %collective-permute-start) | collective-permute-done | bytes 328992 | tf_op jit(solution)/shard_map/ppermute | solution.py:35
  39.9 0.0 collective-permute-start.4
  39.9 0.0 collective-permute-done.17.refs_19_
  39.9 3.5 %collective-permute-start.1 = (bf16[257,640]{1,0:T(8,128)(2,1)S(1)}, bf16[257,640]{1,0:T(8,128)(2,1)}, u32[]{:S(2)}, u32[]{:S(2)}) collective-permute-start(bf16[257,640]{1,0:T(8,128)(2,1)S(1)} %collective-permute-done.refs_1_), channel_id=1, source_target_pairs={{0,28},{2,30},{4,0},{6,2},{8,4},{10,6},{12,8},{14,10},{16,12},{18,... | collective-permute-start | bytes 986888 | tf_op jit(solution)/shard_map/ppermute | solution.py:35
  43.5 0.0 copy-done.9
  43.5 0.0 copy-start.1
  43.5 7.2 %collective-permute-done.4.refs_6_ = bf16[257,640]{1,0:T(8,128)(2,1)S(1)} collective-permute-done((bf16[257,640]{1,0:T(8,128)(2,1)S(1)}, bf16[257,640]{1,0:T(8,128)(2,1)S(1)}, u32[]{:S(2)}, u32[]{:S(2)}) %collective-permute-start.4) | collective-permute-done | bytes 328992 | tf_op jit(solution)/shard_map/ppermute | solution.py:35
  50.7 0.2 collective-permute-start.11
  50.9 0.0 collective-permute-done.1.refs_2_
  50.9 1.3 %collective-permute-start.5 = (bf16[257,640]{1,0:T(8,128)(2,1)S(1)}, bf16[257,640]{1,0:T(8,128)(2,1)S(1)}, u32[]{:S(2)}, u32[]{:S(2)}) collective-permute-start(bf16[257,640]{1,0:T(8,128)(2,1)S(1)} %collective-permute-done.4.refs_6_), channel_id=1, source_target_pairs={{0,4},{2,6},{4,8},{6,10},{8,12},{10,14},{12,16},{14,18},{16,20},{1... | collective-permute-start | bytes 986888 | tf_op jit(solution)/shard_map/ppermute | solution.py:35
  52.2 6.6 %collective-permute-done.11.refs_9_ = bf16[4,248,256]{2,1,0:T(8,128)(2,1)S(1)} collective-permute-done((bf16[4,248,256]{2,1,0:T(8,128)(2,1)S(1)}, bf16[4,248,256]{2,1,0:T(8,128)(2,1)S(1)}, u32[]{:S(2)}, u32[]{:S(2)}) %collective-permute-start.11) | collective-permute-done | bytes 507936 | tf_op jit(solution)/shard_map/ppermute | solution.py:35
  58.9 1.3 %collective-permute-start.2 = (bf16[257,640]{1,0:T(8,128)(2,1)}, bf16[257,640]{1,0:T(8,128)(2,1)S(1)}, u32[]{:S(2)}, u32[]{:S(2)}) collective-permute-start(bf16[257,640]{1,0:T(8,128)(2,1)} %collective-permute-done.1.refs_2_), channel_id=1, source_target_pairs={{0,28},{2,30},{4,0},{6,2},{8,4},{10,6},{12,8},{14,10},{16,12},{18,... | collective-permute-start | bytes 986888 | tf_op jit(solution)/shard_map/ppermute | solution.py:35
  60.2 0.0 collective-permute-done.5.refs_5_
  60.2 0.0 copy-done.10
  60.2 0.0 copy-done.5
  60.2 0.0 copy-done.11
  60.2 0.0 copy-done.6
  60.2 0.0 copy-start.2
  60.2 0.1 collective-permute-start.12
  60.3 4.8 %collective-permute-done.2.refs_3_ = bf16[257,640]{1,0:T(8,128)(2,1)S(1)} collective-permute-done((bf16[257,640]{1,0:T(8,128)(2,1)}, bf16[257,640]{1,0:T(8,128)(2,1)S(1)}, u32[]{:S(2)}, u32[]{:S(2)}) %collective-permute-start.2) | collective-permute-done | bytes 328992 | tf_op jit(solution)/shard_map/ppermute | solution.py:35
  65.1 2.7 %collective-permute-start.13 = (bf16[4,248,256]{2,1,0:T(8,128)(2,1)}, bf16[4,248,256]{2,1,0:T(8,128)(2,1)S(1)}, u32[]{:S(2)}, u32[]{:S(2)}) collective-permute-start(bf16[4,248,256]{2,1,0:T(8,128)(2,1)} %copy-done.6), channel_id=1, source_target_pairs={{0,192},{2,35},{4,196},{6,39},{8,200},{10,43},{12,204},{14,47},{16... | collective-permute-start | bytes 1523720 | tf_op jit(solution)/shard_map/ppermute | solution.py:35
  67.8 0.1 broadcast_select_fusion
  67.9 1.9 %collective-permute-done.12.refs_10_ = bf16[4,248,256]{2,1,0:T(8,128)(2,1)} collective-permute-done((bf16[4,248,256]{2,1,0:T(8,128)(2,1)S(1)}, bf16[4,248,256]{2,1,0:T(8,128)(2,1)}, u32[]{:S(2)}, u32[]{:S(2)}) %collective-permute-start.12) | collective-permute-done | bytes 507936 | tf_op jit(solution)/shard_map/ppermute | solution.py:35
  69.7 1.2 %collective-permute-start.6 = (bf16[257,640]{1,0:T(8,128)(2,1)S(1)}, bf16[257,640]{1,0:T(8,128)(2,1)S(1)}, u32[]{:S(2)}, u32[]{:S(2)}) collective-permute-start(bf16[257,640]{1,0:T(8,128)(2,1)S(1)} %broadcast_select_fusion), channel_id=1, source_target_pairs={{0,4},{2,30},{4,8},{6,2},{8,12},{10,6},{12,16},{14,10},{16,20},{18... | collective-permute-start | bytes 986888 | tf_op jit(solution)/shard_map/ppermute | solution.py:35
  70.9 0.0 copy-done.13
  70.9 0.0 copy-done.14
  70.9 0.0 copy-done.15
  70.9 0.1 pad_add_fusion
  71.0 0.5 pad.4.refs_20_
  71.5 2.5 %collective-permute-done.13.refs_11_ = bf16[4,248,256]{2,1,0:T(8,128)(2,1)S(1)} collective-permute-done((bf16[4,248,256]{2,1,0:T(8,128)(2,1)}, bf16[4,248,256]{2,1,0:T(8,128)(2,1)S(1)}, u32[]{:S(2)}, u32[]{:S(2)}) %collective-permute-start.13) | collective-permute-done | bytes 507936 | tf_op jit(solution)/shard_map/ppermute | solution.py:35
  74.1 2.0 %collective-permute-done.6.refs_4_ = bf16[257,640]{1,0:T(8,128)(2,1)S(1)} collective-permute-done((bf16[257,640]{1,0:T(8,128)(2,1)S(1)}, bf16[257,640]{1,0:T(8,128)(2,1)S(1)}, u32[]{:S(2)}, u32[]{:S(2)}) %collective-permute-start.6) | collective-permute-done | bytes 328992 | tf_op jit(solution)/shard_map/ppermute | solution.py:35
  76.1 0.0 collective-permute-done.15.refs_16_
  76.1 0.0 collective-permute-done.16.refs_17_
  76.1 0.0 collective-permute-done.14.refs_15_
  76.1 0.7 copy-done.12
  76.8 11.3 %pair_scores.1 = f32[32,4,16]{2,1,0:T(4,128)} custom-call(bf16[257,640]{1,0:T(8,128)(2,1)} %bitcast.6, bf16[257,640]{1,0:T(8,128)(2,1)} %copy-done.10, bf16[257,640]{1,0:T(8,128)(2,1)} %collective-permute-done.1.refs_2_, bf16[257,640]{1,0:T(8,128)(2,1)} %copy-done.3, bf16[257,640]{1,0:T(8,128)(2,1)} %copy-done.12, bf16[257,640]{1,0:T(8,128)(2,1)} %copy-done.2, ...), custom_call_target="tpu_custom_call" | custom-call | flops 5052825600 | bytes 20971520 | tf_op jit(solution)/shard_map/pair_scores/pallas_call | solution.py:213
  88.2 19.0 %all_to_all.5 = f32[32,4,16]{2,1,0:T(4,128)S(1)} all-to-all(f32[32,4,16]{2,1,0:T(4,128)} %pair_scores.1), channel_id=1, replica_groups=mesh['y'=4,'xlo'=2,'z'=8,'core'=2,'xhi'=2] {'y','xlo','xhi','core'}, dimensions={0} | all-to-all | bytes 16384 | tf_op jit(solution)/shard_map/all_to_all | solution.py:297
  107.2 0.6 reduce_sum.9
  (16 shorter events, 0.1 us)
Async XLA Ops:
  0.0 11.0 %copy-start = (bf16[1,257,3840]{2,1,0:T(8,128)(2,1)S(1)}, bf16[1,257,3840]{2,1,0:T(8,128)(2,1)}, u32[]{:S(2)}) copy-start(bf16[1,257,3840]{2,1,0:T(8,128)(2,1)} %param.12) | copy-start | bytes 5921284
  3.9 22.4 %copy-start.8 = (bf16[1,257,640]{2,1,0:T(8,128)(2,1)S(1)}, bf16[1,257,640]{2,1,0:T(8,128)(2,1)}, u32[]{:S(2)}) copy-start(bf16[1,257,640]{2,1,0:T(8,128)(2,1)} %param.11) | copy-start | bytes 986884
  3.9 23.4 %copy-start.4 = (bf16[2,240,640]{2,1,0:T(8,128)(2,1)S(1)}, bf16[2,240,640]{2,1,0:T(8,128)(2,1)}, u32[]{:S(2)}) copy-start(bf16[2,240,640]{2,1,0:T(8,128)(2,1)} %refs_18_.1) | copy-start | bytes 1843204
  3.9 72.2 %collective-permute-start.16 = (bf16[8,240,640]{2,1,0:T(8,128)(2,1)}, bf16[8,240,640]{2,1,0:T(8,128)(2,1)}, u32[]{:S(2)}, u32[]{:S(2)}) collective-permute-start(bf16[8,240,640]{2,1,0:T(8,128)(2,1)} %train_grad.5.refs_14_), channel_id=1, source_target_pairs={{0,2},{2,0},{4,6},{6,4},{8,10},{10,8},{12,14},{14,12},{16,18},{18,... | collective-permute-start | bytes 7372808 | tf_op jit(solution)/shard_map/ppermute | solution.py:35
  10.9 65.2 %collective-permute-start.14 = (bf16[8,240,640]{2,1,0:T(8,128)(2,1)}, bf16[8,240,640]{2,1,0:T(8,128)(2,1)}, u32[]{:S(2)}, u32[]{:S(2)}) collective-permute-start(bf16[8,240,640]{2,1,0:T(8,128)(2,1)} %train_grad.3.refs_12_), channel_id=1, source_target_pairs={{0,2},{2,0},{4,6},{6,4},{8,10},{10,8},{12,14},{14,12},{16,18},{18,... | collective-permute-start | bytes 7372808 | tf_op jit(solution)/shard_map/ppermute | solution.py:35
  11.2 9.7 %collective-permute-start.7 = (bf16[248,256]{1,0:T(8,128)(2,1)S(1)}, bf16[248,256]{1,0:T(8,128)(2,1)S(1)}, u32[]{:S(2)}, u32[]{:S(2)}) collective-permute-start(bf16[248,256]{1,0:T(8,128)(2,1)S(1)} %pack.1), channel_id=1, source_target_pairs={{0,0},{2,18},{4,4},{6,22},{8,8},{10,26},{12,12},{14,30},{16,16},{1... | collective-permute-start | bytes 380936 | tf_op jit(solution)/shard_map/ppermute | solution.py:35
  20.9 5.4 %collective-permute-start.10 = (bf16[248,256]{1,0:T(8,128)(2,1)S(1)}, bf16[248,256]{1,0:T(8,128)(2,1)S(1)}, u32[]{:S(2)}, u32[]{:S(2)}) collective-permute-start(bf16[248,256]{1,0:T(8,128)(2,1)S(1)} %collective-permute-done.7.refs_0_), channel_id=1, source_target_pairs={{0,1},{2,130},{4,5},{6,134},{8,9},{10,138},{12,13},{14,142},{16,17... | collective-permute-start | bytes 380936 | tf_op jit(solution)/shard_map/ppermute | solution.py:35
  20.9 6.3 %collective-permute-start.9 = (bf16[248,256]{1,0:T(8,128)(2,1)S(1)}, bf16[248,256]{1,0:T(8,128)(2,1)S(1)}, u32[]{:S(2)}, u32[]{:S(2)}) collective-permute-start(bf16[248,256]{1,0:T(8,128)(2,1)S(1)} %collective-permute-done.7.refs_0_), channel_id=1, source_target_pairs={{0,32},{2,66},{4,36},{6,70},{8,40},{10,74},{12,44},{14,78},{16,48}... | collective-permute-start | bytes 380936 | tf_op jit(solution)/shard_map/ppermute | solution.py:35
  24.0 5.4 %collective-permute-start.8 = (bf16[248,256]{1,0:T(8,128)(2,1)S(1)}, bf16[248,256]{1,0:T(8,128)(2,1)S(1)}, u32[]{:S(2)}, u32[]{:S(2)}) collective-permute-start(bf16[248,256]{1,0:T(8,128)(2,1)S(1)} %collective-permute-done.7.refs_0_), channel_id=1, source_target_pairs={{0,33},{2,194},{4,37},{6,198},{8,41},{10,202},{12,45},{14,206},{16... | collective-permute-start | bytes 380936 | tf_op jit(solution)/shard_map/ppermute | solution.py:35
  26.3 44.6 %copy-start.13 = (s32[22]{0:T(128)S(1)}, s32[22]{0:T(128)}, u32[]{:S(2)}) copy-start(s32[22]{0:T(128)} %param.10) | copy-start | bytes 268
  26.3 44.6 %copy-start.14 = (s32[16]{0:T(128)S(1)}, s32[16]{0:T(128)}, u32[]{:S(2)}) copy-start(s32[16]{0:T(128)} %param.13) | copy-start | bytes 196
  26.3 44.6 %copy-start.15 = (s32[16]{0:T(128)S(1)}, s32[16]{0:T(128)}, u32[]{:S(2)}) copy-start(s32[16]{0:T(128)} %param.15) | copy-start | bytes 196
  26.3 12.0 %collective-permute-start.3 = (bf16[257,640]{1,0:T(8,128)(2,1)S(1)}, bf16[257,640]{1,0:T(8,128)(2,1)S(1)}, u32[]{:S(2)}, u32[]{:S(2)}) collective-permute-start(bf16[257,640]{1,0:T(8,128)(2,1)S(1)} %bitcast.7), channel_id=1, source_target_pairs={{0,4},{2,6},{4,8},{6,10},{8,12},{10,14},{12,16},{14,18},{16,20},{1... | collective-permute-start | bytes 986888 | tf_op jit(solution)/shard_map/ppermute | solution.py:35
  27.3 12.7 %collective-permute-start.17 = (bf16[2,240,640]{2,1,0:T(8,128)(2,1)S(1)}, bf16[2,240,640]{2,1,0:T(8,128)(2,1)S(1)}, u32[]{:S(2)}, u32[]{:S(2)}) collective-permute-start(bf16[2,240,640]{2,1,0:T(8,128)(2,1)S(1)} %copy-done.4), channel_id=1, source_target_pairs={{0,2},{2,0},{4,6},{6,4},{8,10},{10,8},{12,14},{14,12},{16,18},{18,... | collective-permute-start | bytes 1843208 | tf_op jit(solution)/shard_map/ppermute | solution.py:35
  29.4 10.6 %collective-permute-start = (bf16[257,640]{1,0:T(8,128)(2,1)S(1)}, bf16[257,640]{1,0:T(8,128)(2,1)S(1)}, u32[]{:S(2)}, u32[]{:S(2)}) collective-permute-start(bf16[257,640]{1,0:T(8,128)(2,1)S(1)} %bitcast.8), channel_id=1, source_target_pairs={{0,28},{2,30},{4,0},{6,2},{8,4},{10,6},{12,8},{14,10},{16,12},{18,... | collective-permute-start | bytes 986888 | tf_op jit(solution)/shard_map/ppermute | solution.py:35
  38.3 5.2 %copy-start.9 = (bf16[257,640]{1,0:T(8,128)(2,1)}, bf16[257,640]{1,0:T(8,128)(2,1)S(1)}, u32[]{:S(2)}) copy-start(bf16[257,640]{1,0:T(8,128)(2,1)S(1)} %collective-permute-done.3.refs_7_) | copy-start | bytes 986884
  38.3 37.8 %collective-permute-start.15 = (bf16[6,240,640]{2,1,0:T(8,128)(2,1)}, bf16[6,240,640]{2,1,0:T(8,128)(2,1)}, u32[]{:S(2)}, u32[]{:S(2)}) collective-permute-start(bf16[6,240,640]{2,1,0:T(8,128)(2,1)} %train_grad.4.refs_13_), channel_id=1, source_target_pairs={{0,2},{2,0},{4,6},{6,4},{8,10},{10,8},{12,14},{14,12},{16,18},{18,... | collective-permute-start | bytes 5529608 | tf_op jit(solution)/shard_map/ppermute | solution.py:35
  39.9 20.2 %copy-start.10 = (bf16[257,640]{1,0:T(8,128)(2,1)}, bf16[257,640]{1,0:T(8,128)(2,1)S(1)}, u32[]{:S(2)}) copy-start(bf16[257,640]{1,0:T(8,128)(2,1)S(1)} %collective-permute-done.refs_1_) | copy-start | bytes 986884
  39.9 10.8 %collective-permute-start.4 = (bf16[257,640]{1,0:T(8,128)(2,1)S(1)}, bf16[257,640]{1,0:T(8,128)(2,1)S(1)}, u32[]{:S(2)}, u32[]{:S(2)}) collective-permute-start(bf16[257,640]{1,0:T(8,128)(2,1)S(1)} %collective-permute-done.3.refs_7_), channel_id=1, source_target_pairs={{0,4},{2,6},{4,8},{6,10},{8,12},{10,14},{12,16},{14,18},{16,20},{1... | collective-permute-start | bytes 986888 | tf_op jit(solution)/shard_map/ppermute | solution.py:35
  39.9 20.2 %copy-start.5 = (bf16[2,240,640]{2,1,0:T(8,128)(2,1)}, bf16[2,240,640]{2,1,0:T(8,128)(2,1)S(1)}, u32[]{:S(2)}) copy-start(bf16[2,240,640]{2,1,0:T(8,128)(2,1)S(1)} %collective-permute-done.17.refs_19_) | copy-start | bytes 1843204
  39.9 10.9 %collective-permute-start.1 = (bf16[257,640]{1,0:T(8,128)(2,1)S(1)}, bf16[257,640]{1,0:T(8,128)(2,1)}, u32[]{:S(2)}, u32[]{:S(2)}) collective-permute-start(bf16[257,640]{1,0:T(8,128)(2,1)S(1)} %collective-permute-done.refs_1_), channel_id=1, source_target_pairs={{0,28},{2,30},{4,0},{6,2},{8,4},{10,6},{12,8},{14,10},{16,12},{18,... | collective-permute-start | bytes 986888 | tf_op jit(solution)/shard_map/ppermute | solution.py:35
  43.5 32.6 %copy-start.1 = (bf16[4,248,256]{2,1,0:T(8,128)(2,1)}, bf16[4,248,256]{2,1,0:T(8,128)(2,1)S(1)}, u32[]{:S(2)}) copy-start(bf16[4,248,256]{2,1,0:T(8,128)(2,1)S(1)} %stack.1.refs_8_) | copy-start | bytes 1523716
  50.7 9.5 %copy-start.11 = (bf16[257,640]{1,0:T(8,128)(2,1)}, bf16[257,640]{1,0:T(8,128)(2,1)S(1)}, u32[]{:S(2)}) copy-start(bf16[257,640]{1,0:T(8,128)(2,1)S(1)} %collective-permute-done.4.refs_6_) | copy-start | bytes 986884
  50.7 8.2 %collective-permute-start.11 = (bf16[4,248,256]{2,1,0:T(8,128)(2,1)S(1)}, bf16[4,248,256]{2,1,0:T(8,128)(2,1)S(1)}, u32[]{:S(2)}, u32[]{:S(2)}) collective-permute-start(bf16[4,248,256]{2,1,0:T(8,128)(2,1)S(1)} %stack.1.refs_8_), channel_id=1, source_target_pairs={{0,192},{2,35},{4,196},{6,39},{8,200},{10,43},{12,204},{14,47},{16... | collective-permute-start | bytes 1523720 | tf_op jit(solution)/shard_map/ppermute | solution.py:35
  50.9 9.3 %collective-permute-start.5 = (bf16[257,640]{1,0:T(8,128)(2,1)S(1)}, bf16[257,640]{1,0:T(8,128)(2,1)S(1)}, u32[]{:S(2)}, u32[]{:S(2)}) collective-permute-start(bf16[257,640]{1,0:T(8,128)(2,1)S(1)} %collective-permute-done.4.refs_6_), channel_id=1, source_target_pairs={{0,4},{2,6},{4,8},{6,10},{8,12},{10,14},{12,16},{14,18},{16,20},{1... | collective-permute-start | bytes 986888 | tf_op jit(solution)/shard_map/ppermute | solution.py:35
  58.9 1.3 %copy-start.6 = (bf16[4,248,256]{2,1,0:T(8,128)(2,1)}, bf16[4,248,256]{2,1,0:T(8,128)(2,1)S(1)}, u32[]{:S(2)}) copy-start(bf16[4,248,256]{2,1,0:T(8,128)(2,1)S(1)} %collective-permute-done.11.refs_9_) | copy-start | bytes 1523716
  58.9 6.2 %collective-permute-start.2 = (bf16[257,640]{1,0:T(8,128)(2,1)}, bf16[257,640]{1,0:T(8,128)(2,1)S(1)}, u32[]{:S(2)}, u32[]{:S(2)}) collective-permute-start(bf16[257,640]{1,0:T(8,128)(2,1)} %collective-permute-done.1.refs_2_), channel_id=1, source_target_pairs={{0,28},{2,30},{4,0},{6,2},{8,4},{10,6},{12,8},{14,10},{16,12},{18,... | collective-permute-start | bytes 986888 | tf_op jit(solution)/shard_map/ppermute | solution.py:35
  60.2 15.9 %copy-start.2 = (bf16[257,640]{1,0:T(8,128)(2,1)}, bf16[257,640]{1,0:T(8,128)(2,1)S(1)}, u32[]{:S(2)}) copy-start(bf16[257,640]{1,0:T(8,128)(2,1)S(1)} %collective-permute-done.5.refs_5_) | copy-start | bytes 986884
  60.2 9.5 %collective-permute-start.12 = (bf16[4,248,256]{2,1,0:T(8,128)(2,1)S(1)}, bf16[4,248,256]{2,1,0:T(8,128)(2,1)}, u32[]{:S(2)}, u32[]{:S(2)}) collective-permute-start(bf16[4,248,256]{2,1,0:T(8,128)(2,1)S(1)} %stack.1.refs_8_), channel_id=1, source_target_pairs={{0,64},{2,34},{4,68},{6,38},{8,72},{10,42},{12,76},{14,46},{16,80}... | collective-permute-start | bytes 1523720 | tf_op jit(solution)/shard_map/ppermute | solution.py:35
  65.1 11.0 %copy-start.3 = (bf16[257,640]{1,0:T(8,128)(2,1)}, bf16[257,640]{1,0:T(8,128)(2,1)S(1)}, u32[]{:S(2)}) copy-start(bf16[257,640]{1,0:T(8,128)(2,1)S(1)} %collective-permute-done.2.refs_3_) | copy-start | bytes 986884
  65.1 8.9 %collective-permute-start.13 = (bf16[4,248,256]{2,1,0:T(8,128)(2,1)}, bf16[4,248,256]{2,1,0:T(8,128)(2,1)S(1)}, u32[]{:S(2)}, u32[]{:S(2)}) collective-permute-start(bf16[4,248,256]{2,1,0:T(8,128)(2,1)} %copy-done.6), channel_id=1, source_target_pairs={{0,192},{2,35},{4,196},{6,39},{8,200},{10,43},{12,204},{14,47},{16... | collective-permute-start | bytes 1523720 | tf_op jit(solution)/shard_map/ppermute | solution.py:35
  69.7 6.3 %collective-permute-start.6 = (bf16[257,640]{1,0:T(8,128)(2,1)S(1)}, bf16[257,640]{1,0:T(8,128)(2,1)S(1)}, u32[]{:S(2)}, u32[]{:S(2)}) collective-permute-start(bf16[257,640]{1,0:T(8,128)(2,1)S(1)} %broadcast_select_fusion), channel_id=1, source_target_pairs={{0,4},{2,30},{4,8},{6,2},{8,12},{10,6},{12,16},{14,10},{16,20},{18... | collective-permute-start | bytes 986888 | tf_op jit(solution)/shard_map/ppermute | solution.py:35
  74.1 2.1 %copy-start.7 = (bf16[4,248,256]{2,1,0:T(8,128)(2,1)}, bf16[4,248,256]{2,1,0:T(8,128)(2,1)S(1)}, u32[]{:S(2)}) copy-start(bf16[4,248,256]{2,1,0:T(8,128)(2,1)S(1)} %collective-permute-done.13.refs_11_) | copy-start | bytes 1523716
  76.1 0.7 copy-start.12
